TPU v7x, 128 devices: a whole 4x4x4 slice. The times are simulated.
128 devices in a mesh: dp: 1, cp: 128 (over z, y, x, core).
Axes of the slice: x: 4, y: 4, z: 4, core: 2. Of those that a mesh axis runs over, the one named last changes fastest.
Arguments:
- query: bfloat16 [6, 4096, 16, 128], P('dp', 'cp')
- key: bfloat16 [6, 4096, 128], P('dp', 'cp')
- value: bfloat16 [6, 4096, 128], P('dp', 'cp')
- positions: int32 [4096], P(('dp', 'cp'))
- grad_out: bfloat16 [6, 4096, 16, 128], P('dp', 'cp')
Outputs:
- output 1: bfloat16 [6, 4096, 16, 128], P('dp', 'cp')
- output 2: bfloat16 [6, 4096, 16, 128], P('dp', 'cp')
- output 3: bfloat16 [6, 4096, 128], P('dp', 'cp')
- output 4: bfloat16 [6, 4096, 128], P('dp', 'cp')
All inputs are finite; a program needn't handle non-finite values.
Results may differ from a plain program's by a relative error of at most 0.00808827.
Values are sent between devices in bfloat16 or wider.
A program may use at most 1 GiB of HBM per device.

v0:
```python
import jax
import jax.numpy as jnp
from jax import lax
from jax.sharding import PartitionSpec as P

ROPE_BASE = 10000


def rope_tables(positions, head):
    half_dim = head // 2
    inv_freq = jnp.power(jnp.float32(ROPE_BASE), -2.0 * jnp.arange(half_dim, dtype=jnp.float32) / head)
    angles = positions.astype(jnp.float32)[..., None] * inv_freq
    angles = jnp.concatenate([angles, angles], axis=-1)
    return jnp.cos(angles), jnp.sin(angles)


def rotate(values, cos_tab, sin_tab):
    half_dim = values.shape[-1] // 2
    turned = jnp.concatenate([-values[..., half_dim:], values[..., :half_dim]], axis=-1)
    return values * cos_tab + turned * sin_tab


def solution(mesh):
    cp_size = mesh.shape['cp']
    shift_pairs = [(source, (source + 1) % cp_size) for source in range(cp_size)]
    query_spec = P('dp', 'cp', None, None)
    kv_spec = P('dp', 'cp', None)
    pos_spec = P(('dp', 'cp'))

    def per_device(query, key, value, positions, grad_out):
        batch, blk_len, heads, head = query.shape
        scale = head ** -0.5
        my_idx = lax.axis_index('cp')
        cos_tab, sin_tab = rope_tables(positions, head)
        cos_q = cos_tab[None, :, None, :]
        sin_q = sin_tab[None, :, None, :]
        query_rot = rotate(query, cos_q, sin_q).astype(jnp.bfloat16)
        key_rot = rotate(key, cos_tab[None], sin_tab[None]).astype(jnp.bfloat16)
        local_idx = jnp.arange(blk_len)
        diag_mask = (local_idx[None, :] <= local_idx[:, None])[None, :, None, :]

        def block_scores(key_blk, causal_mask):
            scores = jnp.einsum('crie,cle->cril', query_rot, key_blk, preferred_element_type=jnp.float32) * scale
            if causal_mask is None:
                return scores
            return jnp.where(causal_mask, scores, -jnp.inf)

        def forward_block(key_blk, value_blk, state, causal_mask):
            run_max, run_sum, out_acc = state
            scores = block_scores(key_blk, causal_mask)
            new_max = jnp.maximum(run_max, jnp.max(scores, axis=-1))
            factor = jnp.exp(run_max - new_max)
            weights = jnp.exp(scores - new_max[..., None])
            run_sum = run_sum * factor + jnp.sum(weights, axis=-1)
            out_acc = out_acc * factor[..., None] + jnp.einsum('cril,cle->crie', weights.astype(jnp.bfloat16), value_blk, preferred_element_type=jnp.float32)
            return new_max, run_sum, out_acc

        init_state = (jnp.full((batch, blk_len, heads), -jnp.inf, jnp.float32), jnp.zeros((batch, blk_len, heads), jnp.float32), jnp.zeros((batch, blk_len, heads, head), jnp.float32))
        state = forward_block(key_rot, value, init_state, diag_mask)

        def forward_step(step, carry):
            key_blk, value_blk, state_in = carry
            key_blk, value_blk = lax.ppermute((key_blk, value_blk), 'cp', shift_pairs)
            state_out = lax.cond(step <= my_idx, lambda prev: forward_block(key_blk, value_blk, prev, None), lambda prev: prev, state_in)
            return key_blk, value_blk, state_out

        fwd_carry = lax.fori_loop(1, cp_size, forward_step, (key_rot, value, state))
        run_max, run_sum, out_acc = fwd_carry[2]
        attn_out = (out_acc / run_sum[..., None]).astype(jnp.bfloat16)
        log_sum = run_max + jnp.log(run_sum)
        delta = jnp.einsum('bqhd,bqhd->bqh', grad_out, attn_out, preferred_element_type=jnp.float32)

        def backward_block(key_blk, value_blk, grads, causal_mask):
            dquery_acc, dkey_blk, dvalue_blk = grads
            scores = block_scores(key_blk, causal_mask)
            probs_f = jnp.exp(scores - log_sum[..., None])
            dprobs = jnp.einsum('crie,cle->cril', grad_out, value_blk, preferred_element_type=jnp.float32)
            dscore = (probs_f * (dprobs - delta[..., None])).astype(jnp.bfloat16)
            dquery_acc = dquery_acc + jnp.einsum('cril,cle->crie', dscore, key_blk, preferred_element_type=jnp.float32) * scale
            dkey_blk = dkey_blk + jnp.einsum('cril,crie->cle', dscore, query_rot, preferred_element_type=jnp.float32) * scale
            dvalue_blk = dvalue_blk + jnp.einsum('cril,crie->cle', probs_f.astype(jnp.bfloat16), grad_out, preferred_element_type=jnp.float32)
            return dquery_acc, dkey_blk, dvalue_blk

        zero_kv = jnp.zeros((batch, blk_len, head), jnp.float32)
        grads = backward_block(key_rot, value, (jnp.zeros((batch, blk_len, heads, head), jnp.float32), zero_kv, zero_kv), diag_mask)

        def backward_step(step, carry):
            key_blk, value_blk, dquery_acc, dkey_blk, dvalue_blk = carry
            key_blk, value_blk, dkey_blk, dvalue_blk = lax.ppermute((key_blk, value_blk, dkey_blk, dvalue_blk), 'cp', shift_pairs)
            grads_new = lax.cond(step <= my_idx, lambda prev: backward_block(key_blk, value_blk, prev, None), lambda prev: prev, (dquery_acc, dkey_blk, dvalue_blk))
            return (key_blk, value_blk) + tuple(grads_new)

        bwd_carry = lax.fori_loop(1, cp_size, backward_step, (key_rot, value) + tuple(grads))
        dkey_home, dvalue_home = lax.ppermute((bwd_carry[3], bwd_carry[4]), 'cp', shift_pairs)
        grad_query = rotate(bwd_carry[2], cos_q, -sin_q).astype(jnp.bfloat16)
        grad_key = rotate(dkey_home, cos_tab[None], -sin_tab[None]).astype(jnp.bfloat16)
        return attn_out, grad_query, grad_key, dvalue_home.astype(jnp.bfloat16)

    return jax.shard_map(per_device, mesh=mesh, in_specs=(query_spec, kv_spec, kv_spec, pos_spec, query_spec), out_specs=(query_spec, query_spec, kv_spec, kv_spec), check_vma=False)
```

profile of v0, /device:TPU:96, one launch (start us, length us, event | category | flops | bytes accessed | tf_op | source)
XLA Modules:
  0.0 3402.6 jit_solution(2375313362529892506)
XLA Ops:
  10.5 1380.2 %while.42 = (s32[]{:T(128)}, bf16[6,32,128]{2,1,0:T(8,128)(2,1)S(1)}, bf16[6,32,128]{2,1,0:T(8,128)(2,1)S(1)}, f32[6,32,16]{2,1,0:T(8,128)S(1)}, f32[6,32,16]{2,...) while((s32[]{:T(128)}, ...), condition=%wide.region_7.8_spmd, body=%wide.region_2.7_spmd.sunk | while | flops 51714052 | bytes 5996835 | solution.py:67
  1399.7 1992.6 %while.43 = (s32[]{:T(128)}, bf16[6,32,128]{2,1,0:T(8,128)(2,1)S(1)}, bf16[6,32,128]{2,1,0:T(8,128)(2,1)}, f32[6,32,16,128]{3,2,1,0:T(8,128)S(1)}, f32[6,32,128]...) while((s32[]{:T(128)}, ...), condition=%wide.region_11.12_spmd, body=%wide.region_8.11_spmd.sunk | while | flops 127279104 | bytes 13541823 | solution.py:93
  1416.7 9.7 collective-permute-done.2
  1433.5 9.7 collective-permute-done.2
  1450.3 9.7 collective-permute-done.2
  1467.1 9.7 collective-permute-done.2
  1483.9 9.7 collective-permute-done.2
  1500.7 9.7 collective-permute-done.2
  1517.5 9.7 collective-permute-done.2
  1534.2 9.7 collective-permute-done.2
  1551.0 9.7 collective-permute-done.2
  1567.8 9.7 collective-permute-done.2
  1584.6 9.7 collective-permute-done.2
  1601.4 9.7 collective-permute-done.2
  1618.2 9.7 collective-permute-done.2
  1635.0 9.7 collective-permute-done.2
  1651.8 9.7 collective-permute-done.2
  1668.6 9.7 collective-permute-done.2
  1685.4 9.7 collective-permute-done.2
  1702.2 9.7 collective-permute-done.2
  1718.9 9.7 collective-permute-done.2
  1870.1 9.7 collective-permute-done.2
  1886.9 9.7 collective-permute-done.2
  2189.1 9.7 collective-permute-done.2
  2205.9 9.7 collective-permute-done.2
  2508.2 9.7 collective-permute-done.2
  2524.9 9.7 collective-permute-done.2
  2827.2 9.7 collective-permute-done.2
  2844.0 9.7 collective-permute-done.2
  3134.7 9.7 collective-permute-done.2
  3208.3 9.7 collective-permute-done.2
  3367.9 9.7 collective-permute-done.2
  (3809 shorter events, 3839.9 us)
Async XLA Ops:
  1399.7 11.1 collective-permute-start.4
  1416.6 11.0 collective-permute-start.5
  1567.7 11.0 collective-permute-start.5
  1584.5 11.0 collective-permute-start.5
  1601.3 11.0 collective-permute-start.4
  1601.3 11.0 collective-permute-start.5
  1618.1 11.0 collective-permute-start.4
  1618.1 11.0 collective-permute-start.5
  1634.9 11.0 collective-permute-start.4
  1634.9 11.0 collective-permute-start.5
  1651.7 11.0 collective-permute-start.4
  1668.5 11.0 collective-permute-start.4
  1886.8 11.0 collective-permute-start.5
  1903.6 11.0 collective-permute-start.5
  1920.3 11.0 collective-permute-start.4
  1920.3 11.0 collective-permute-start.5
  1937.1 11.0 collective-permute-start.4
  1937.1 11.0 collective-permute-start.5
  1953.9 11.0 collective-permute-start.4
  1953.9 11.0 collective-permute-start.5
  1970.7 11.0 collective-permute-start.4
  1987.5 11.0 collective-permute-start.4
  2205.8 11.0 collective-permute-start.5
  2222.6 11.0 collective-permute-start.5
  2239.4 11.0 collective-permute-start.4
  2239.4 11.0 collective-permute-start.5
  2256.2 11.0 collective-permute-start.4
  2256.2 11.0 collective-permute-start.5
  2273.0 11.0 collective-permute-start.4
  2273.0 11.0 collective-permute-start.5
  2289.8 11.0 collective-permute-start.4
  2306.6 11.0 collective-permute-start.4
  (837 other events, 8559.7 us)
where the time goes:
time: 3410 us; the launch traced here: 3400 us
  waiting for transfers between devices  2340 us (69%)
  matrix products  589 us (17%)
  local copies, waits for them, and re-layouts  313 us (9%)
  other arithmetic  106 us (3%)
    ppermute x508, waiting for transfers between devices, backward_step(): lax.ppermute((key_blk, value_blk, dkey_blk, dvalue_blk), 'cp', shift_pairs)  1300 us
    ppermute x254, waiting for transfers between devices, forward_step(): key_blk, value_blk = lax.ppermute((key_blk, value_blk), 'cp', shift_pairs)  1030 us
    while x762, local copies, waits for them, and re-layouts  243 us
    dot_general x193, matrix products, block_scores(): jnp.einsum('crie,cle->cril', query_rot, key_blk, preferred_element_type=j...  223 us
    dot_general x97, matrix products, forward_block(): jnp.einsum('cril,cle->crie', weights.astype(jnp.bfloat16), value_blk, pre...  159 us
    reduce_sum x97, other arithmetic, forward_block(): run_sum = run_sum * factor + jnp.sum(weights, axis=-1)  88.9 us
  transfers between devices with their start and end apart: 764, of which 509 were waited for; matrix products, arithmetic and copies ran while one was open for 2% of the time, Pallas kernels for 0%

commit v1 on v0

v1 whole, which is shorter than its diff:
```python
import jax
import jax.numpy as jnp
from jax import lax
from jax.experimental import pallas as pl
from jax.experimental.pallas import tpu as pltpu
from jax.sharding import PartitionSpec as PS

ROPE_BASE = 10000
SEQS, HEADS, HEAD, BLK = 6, 16, 128, 32
ROWS = BLK * HEADS
CK = 256
STEPS = 17
NC = 16
UF, UB = 4, 4
SCALE = HEAD ** -0.5
C2 = SCALE * 1.4426950408889634
BIG = 1e30
BF, F32 = jnp.bfloat16, jnp.float32
MESH = pl.DeviceIdType.MESH

PLACE = [int(d, 16) for d in 'E45C2760D389FA1B']
ORDER = [[int(d, 16) for d in row] for row in (
    '530142768E9ADBCF',
    'CD8907162534BAFE',
    'F9E8A54BDC263701',
    'A52B34867901FDCE',
    'F9BAE538201746DC',
    'ABCD452130F867E9')]
PIECES = 4
PP = 16 // PIECES


def _tables():
    work = {}
    dest = [[0] * 16 for _ in range(SEQS)]
    limit = {}
    slots = {}
    for s in range(SEQS):
        for i, j in enumerate(ORDER[s]):
            q = 16 * (s % 3) + i
            f, g = divmod(q, 3)
            big_c = 8 * (s // 3) + f // 2
            slot = s % 3 - (6 * (f // 2)) // 16
            slots[big_c, s] = slot
            work[PLACE[big_c], f % 2, g] = (s, j, slot)
            dest[s][j] = PLACE[big_c] * 8 + (f % 2) * 4 + g
            limit[big_c, s] = max(limit.get((big_c, s), 0), ((31 - j) // 2) // PP)
    chips = [[(PLACE[c], slots[c, t], limit[c, t]) for (c, t) in sorted(slots) if t == s] for s in range(SEQS)]
    lim = [[-1] * 16, [-1] * 16]
    seq = [[0] * 16, [0] * 16]
    nth = [[0] * 16, [0] * 16]
    for s in range(SEQS):
        for n, (place, slot, last) in enumerate(chips[s]):
            lim[slot][place], seq[slot][place], nth[slot][place] = last, s, n
    meta = []
    for p in range(32):
        w = [work[p // 2, p % 2, g] for g in range(3)]
        meta.append([t[1] for t in w] + [t[2] for t in w] + [2 if lim[1][p // 2] >= 0 else 1] + [t[0] for t in w])
    return dest, chips, lim, seq, nth, meta


DEST, CHIPS, LIM, SEQ, NTH, META = _tables()
NCH = max(len(c) for c in CHIPS)


def lut(index, table):
    value = jnp.int32(table[0])
    for n in range(1, len(table)):
        if table[n] != table[n - 1]:
            value = jnp.where(index >= n, jnp.int32(table[n]), value)
    return value


def place_of():
    me = lax.axis_index('cp')
    return me, me % 2, (me // 2) % 4, me // 8


def send(src, dst, ssem, rsem, dev, me):
    @pl.when(dev != me)
    def _():
        pltpu.make_async_remote_copy(src, dst, ssem, rsem, device_id={'cp': dev}, device_id_type=MESH).start()

    @pl.when(dev == me)
    def _():
        pltpu.make_async_copy(src, dst, rsem).start()


def landed(ref, sem):
    pltpu.make_async_copy(ref, ref, sem).wait()


def exchange_in(q, do, kv, cs, qr, dor, csr, kvr, ts, tr, s1, r1, s2, r2, s3, r3):
    me, c, x, place = place_of()
    p = 2 * place + c
    j = jnp.minimum(p, 31 - p)
    hi = p // 16
    lims = [lut(place, LIM[slot]) for slot in range(2)]
    piece_me = place // PP

    n = 0
    for s in range(SEQS):
        for (chip, slot, last) in CHIPS[s]:
            @pl.when(piece_me <= last)
            def _(s=s, chip=chip, slot=slot, n=n):
                send(kv.at[s], kvr.at[slot, place, x, c], s1.at[n], r1.at[slot, piece_me], chip * 8 + 2 * x + c, me)
            n += 1
    for s in range(SEQS):
        code = lut(j, DEST[s])
        k = 2 * (code % 4) + hi
        dev = (code // 8) * 8 + 2 * x + (code // 4) % 2
        send(q.at[s], qr.at[k], ts.at[s, 0], tr.at[k, 0], dev, me)
        send(do.at[s], dor.at[k], ts.at[s, 1], tr.at[k, 1], dev, me)
        send(cs, csr.at[k], ts.at[s, 2], tr.at[k, 2], dev, me)

    def mine(slot, i, xx, cc):
        return kvr.at[slot, pl.ds(PP * i, PP), xx, cc]

    def both(slot, i, cc):
        return kvr.at[slot, pl.ds(PP * i, PP), :, cc]

    for i in range(PIECES):
        for slot in range(2):
            @pl.when(i <= lims[slot])
            def _(i=i, slot=slot):
                landed(mine(slot, i, x, c), r1.at[slot, i])
                for d in range(1, 4):
                    pltpu.make_async_remote_copy(
                        mine(slot, i, x, c), mine(slot, i, x, c), s2.at[slot, i, d - 1], r2.at[slot, i, d - 1],
                        device_id={'cp': place * 8 + 2 * ((x + d) % 4) + c}, device_id_type=MESH).start()
    for i in range(PIECES):
        for slot in range(2):
            @pl.when(i <= lims[slot])
            def _(i=i, slot=slot):
                for d in range(1, 4):
                    landed(mine(slot, i, (x + 4 - d) % 4, c), r2.at[slot, i, d - 1])
                pltpu.make_async_remote_copy(
                    both(slot, i, c), both(slot, i, c), s3.at[slot, i], r3.at[slot, i],
                    device_id={'cp': me + 1 - 2 * c}, device_id_type=MESH).start()
    for k in range(6):
        landed(qr.at[k], tr.at[k, 0])
        landed(dor.at[k], tr.at[k, 1])
        landed(csr.at[k], tr.at[k, 2])
    for i in range(PIECES):
        for slot in range(2):
            @pl.when(i <= lims[slot])
            def _(i=i, slot=slot):
                landed(both(slot, i, 1 - c), r3.at[slot, i])
                for d in range(1, 4):
                    landed(mine(slot, i, x, c), s2.at[slot, i, d - 1])
                landed(both(slot, i, c), s3.at[slot, i])
    n = 0
    for s in range(SEQS):
        for (chip, slot, last) in CHIPS[s]:
            @pl.when((piece_me <= last) & (place != chip))
            def _(s=s, n=n):
                landed(kv.at[s], s1.at[n])
            n += 1
    for s in range(SEQS):
        code = lut(j, DEST[s])
        dev = (code // 8) * 8 + 2 * x + (code // 4) % 2

        @pl.when(dev != me)
        def _(s=s):
            landed(q.at[s], ts.at[s, 0])
            landed(do.at[s], ts.at[s, 1])
            landed(cs, ts.at[s, 2])


def run_in(q, do, kv, cs):
    dma = pltpu.SemaphoreType.DMA
    n_kv = sum(len(c) for c in CHIPS)
    any_ = pl.BlockSpec(memory_space=pl.ANY)
    return pl.pallas_call(
        exchange_in,
        in_specs=[any_] * 4, out_specs=[any_] * 4,
        out_shape=[
            jax.ShapeDtypeStruct((6, ROWS, HEAD), BF), jax.ShapeDtypeStruct((6, ROWS, HEAD), BF),
            jax.ShapeDtypeStruct((6, BLK, HEAD), F32), jax.ShapeDtypeStruct((2, 16, 4, 2, BLK, 2 * HEAD), BF)],
        scratch_shapes=[dma((6, 3)), dma((6, 3)), dma((n_kv,)), dma((2, PIECES)), dma((2, PIECES, 3)), dma((2, PIECES, 3)),
                        dma((2, PIECES)), dma((2, PIECES))],
        compiler_params=pltpu.CompilerParams(has_side_effects=True, vmem_limit_bytes=63 << 20),
        name='exchange_in')(q, do, kv, cs)


def dot(a, b):
    return jnp.dot(a, b, preferred_element_type=F32)


def dot_nt(a, b):
    return lax.dot_general(a, b, (((1,), (1,)), ((), ())), preferred_element_type=F32)


def max8(v):
    return jnp.broadcast_to(jnp.max(v, axis=0, keepdims=True), (8, ROWS))


def sum8(v):
    return jnp.broadcast_to(jnp.sum(v, axis=0, keepdims=True), (8, ROWS))


def sub8(a, b):
    return a.reshape(-1, 8, ROWS) - b[None]


def turn(v, cs, sign):
    cos = jnp.concatenate([cs[:, :64], cs[:, :64]], axis=1)
    sin = jnp.concatenate([-cs[:, 64:], cs[:, 64:]], axis=1)
    v = v.reshape(BLK, HEADS, HEAD)
    other = jnp.concatenate([v[..., 64:], v[..., :64]], axis=-1)
    if sign > 0:
        out = v * cos[:, None, :] + other * sin[:, None, :]
    else:
        out = v * cos[:, None, :] - other * sin[:, None, :]
    return out.astype(BF).reshape(ROWS, HEAD)


def attend(meta, q_ref, do_ref, cs_ref, kv_ref, o_ref, dq_ref, dkv_ref,
           kt, vt, dkt, dvt, p_ref, mx, qa, dot_t, ot, dqt, mst, lst, dst, dp_ref, mk):
    g = pl.program_id(0)
    xw = meta[7]

    def rows(ch):
        return pl.ds(pl.multiple_of(ch * CK, CK), CK)

    @pl.when(g == 0)
    def _():
        @pl.loop(0, NC * meta[6])
        def _(i):
            s = i // NC
            ch = i % NC
            kt[s, ch] = kv_ref[s, rows(ch), :HEAD].T
            vt[s, ch] = kv_ref[s, rows(ch), HEAD:].T
            dkt[s, ch] = jnp.zeros((HEAD, CK), F32)
            dvt[s, ch] = jnp.zeros((HEAD, CK), F32)
        row = lax.broadcasted_iota(jnp.int32, (HEAD, ROWS), 0)
        col = lax.broadcasted_iota(jnp.int32, (HEAD, ROWS), 1)
        onehot = jnp.where(col // HEADS == row, 1.0, 0.0).astype(BF)
        for tl in range(2):
            qa[tl, HEAD:, :] = onehot
        ki = lax.broadcasted_iota(jnp.int32, (CK, HEAD), 0)
        di = lax.broadcasted_iota(jnp.int32, (CK, HEAD), 1)
        mk[0] = jnp.zeros((CK, HEAD), BF)
        for cc in range(2):
            mk[1 + cc] = jnp.where((di < BLK) & (ki > di + 64 * xw + BLK * cc), -BIG, 0.0).astype(BF)

    j = meta[g]
    slot = meta[3 + g]
    a = j // 2 + 1

    def tlch(i):
        tl = (i >= a).astype(jnp.int32)
        return tl, i - a * tl

    @pl.loop(0, 2)
    def _(tl):
        qa[tl, :HEAD, :] = turn(q_ref[tl].astype(F32), cs_ref[tl], 1).T
        dot_t[tl] = do_ref[tl].T
        ot[tl] = jnp.zeros((HEAD, ROWS), F32)
        dqt[tl] = jnp.zeros((HEAD, ROWS), F32)
        mst[tl] = jnp.full((8, ROWS), -BIG, F32)
        lst[tl] = jnp.zeros((8, ROWS), F32)

    def s_step(i, pb, pu):
        tl, ch = tlch(i)
        diag = ch == jnp.where(tl == 0, a - 1, NC - a)
        sel = jnp.where(diag, 1 + lax.rem(j + tl, 2), 0)
        ka = jnp.concatenate([kv_ref[slot, rows(ch), :HEAD], mk[sel]], axis=1)
        s = dot(ka, qa[tl]) * C2
        p_ref[pb, pu] = s
        mx[i] = jnp.max(s.reshape(CK // 8, 8, ROWS), axis=0)

    def o_step(i, pb, pu):
        tl, ch = tlch(i)
        mo = mst[tl]
        mn = jnp.maximum(mo, max8(mx[i]))
        al = jnp.exp2(mo - mn)
        e = jnp.exp2(sub8(p_ref[pb, pu], mn))
        mst[tl] = mn
        lst[tl] = lst[tl] * al + jnp.sum(e, axis=0)
        ot[tl] = (ot[tl].reshape(-1, 8, ROWS) * al[None]).reshape(HEAD, ROWS) + dot(vt[slot, ch], e.reshape(CK, ROWS).astype(BF))

    s_step(jnp.int32(0), 0, 0)

    @pl.loop(0, 16 // UF)
    def _(b):
        for u in range(UF):
            i = b * UF + u
            s_step(i + 1, b + (u + 1) // UF, (u + 1) % UF)
            o_step(i, b, u)
    o_step(jnp.int32(16), 16 // UF, 0)

    @pl.loop(0, 2)
    def _(tl):
        l = sum8(lst[tl])
        o = (ot[tl].reshape(-1, 8, ROWS) / l[None]).reshape(HEAD, ROWS).astype(BF)
        o_ref[tl] = o.T
        dst[tl] = sum8(jnp.sum((o.astype(F32) * dot_t[tl].astype(F32)).reshape(-1, 8, ROWS), axis=0))
        mst[tl] = mst[tl] + jnp.log2(l)

    def d_step(i, b):
        tl, ch = tlch(i)
        dp_ref[b] = dot(kv_ref[slot, rows(ch), HEAD:], dot_t[tl])

    def g_step(i, b, pb, pu, ahead):
        tl, ch = tlch(i)
        pr = jnp.exp2(sub8(p_ref[pb, pu], mst[tl]))
        prb = pr.reshape(CK, ROWS).astype(BF)
        dvt[slot, ch] += dot_nt(dot_t[tl], prb)
        ahead()
        ds = (pr * sub8(dp_ref[b], dst[tl])).reshape(CK, ROWS).astype(BF)
        dqt[tl] += dot(kt[slot, ch], ds)
        dkt[slot, ch] += dot_nt(qa[tl, :HEAD, :], ds)

    d_step(jnp.int32(0), 0)

    @pl.loop(0, 16 // UB)
    def _(b):
        for u in range(UB):
            i = b * UB + u
            g_step(i, u % 2, b, u, lambda: d_step(i + 1, (u + 1) % 2))
    g_step(jnp.int32(16), 0, 16 // UF, 0, lambda: None)

    @pl.loop(0, 2)
    def _(tl):
        dq_ref[tl] = turn((dqt[tl] * SCALE).T, cs_ref[tl], -1)

    @pl.when(g == 2)
    def _():
        @pl.loop(0, NC * meta[6])
        def _(i):
            s = i // NC
            ch = i % NC
            dkv_ref[s, rows(ch), :HEAD] = dkt[s, ch].T
            dkv_ref[s, rows(ch), HEAD:] = dvt[s, ch].T


def run_attend(meta, q, do, cs, kv):
    tile = pl.BlockSpec((2, ROWS, HEAD), lambda i, _: (i, 0, 0))
    whole = pl.BlockSpec((2, NC * CK, 2 * HEAD), lambda i, _: (0, 0, 0), pipeline_mode=pl.Buffered(1))
    v = pltpu.VMEM
    return pl.pallas_call(
        attend,
        grid_spec=pltpu.PrefetchScalarGridSpec(
            num_scalar_prefetch=1, grid=(3,),
            in_specs=[tile, tile, pl.BlockSpec((2, BLK, HEAD), lambda i, _: (i, 0, 0)), whole],
            out_specs=[tile, tile, whole],
            scratch_shapes=[
                v((2, NC, HEAD, CK), BF), v((2, NC, HEAD, CK), BF), v((2, NC, HEAD, CK), F32), v((2, NC, HEAD, CK), F32),
                v((16 // UF + 1, UF, CK, ROWS), F32), v((STEPS, 8, ROWS), F32), v((2, 2 * HEAD, ROWS), BF), v((2, HEAD, ROWS), BF),
                v((2, HEAD, ROWS), F32), v((2, HEAD, ROWS), F32), v((2, 8, ROWS), F32), v((2, 8, ROWS), F32),
                v((2, 8, ROWS), F32), v((2, CK, ROWS), F32), v((3, CK, HEAD), BF)]),
        out_shape=[jax.ShapeDtypeStruct((6, ROWS, HEAD), BF)] * 2 + [jax.ShapeDtypeStruct((2, NC * CK, 2 * HEAD), F32)],
        compiler_params=pltpu.CompilerParams(vmem_limit_bytes=60 << 20),
        name='attend')(meta, q, do, cs, kv)


def exchange_out(o, dq, dkv, cs, att, gq, gk, gv, own, peer, xr, zs, home,
                 ls, ts, tr, s1, r1, s2, r2, s3, r3):
    me, c, x, place = place_of()
    p = 2 * place + c
    lims = [lut(place, LIM[slot]) for slot in range(2)]
    for k in range(6):
        g, tl = divmod(k, 2)
        s = lut(p, [META[n][7 + g] for n in range(32)])
        j = lut(p, [META[n][g] for n in range(32)])
        src = j if tl == 0 else 31 - j
        dev = (src // 2) * 8 + 2 * x + src % 2
        send(o.at[k], att.at[s], ts.at[k, 0], tr.at[s, 0], dev, me)
        send(dq.at[k], gq.at[s], ts.at[k, 1], tr.at[s, 1], dev, me)

    def part(slot, i):
        return pl.ds(PP * i, PP)

    for i in reversed(range(PIECES)):
        for slot in range(2):
            @pl.when(i <= lims[slot])
            def _(i=i, slot=slot):
                pltpu.make_async_remote_copy(
                    dkv.at[slot, part(slot, i), :, 1 - c], peer.at[slot, part(slot, i)], s1.at[slot, i], r1.at[slot, i],
                    device_id={'cp': me + 1 - 2 * c}, device_id_type=MESH).start()
                pltpu.make_async_copy(dkv.at[slot, part(slot, i), :, c], own.at[slot, part(slot, i)], ls.at[slot, i]).start()
    for i in reversed(range(PIECES)):
        for slot in range(2):
            @pl.when(i <= lims[slot])
            def _(i=i, slot=slot):
                landed(own.at[slot, part(slot, i)], ls.at[slot, i])
                landed(peer.at[slot, part(slot, i)], r1.at[slot, i])
                own[slot, part(slot, i)] += peer[slot, part(slot, i)]
                for d in range(1, 4):
                    pltpu.make_async_remote_copy(
                        own.at[slot, part(slot, i), (x + d) % 4], xr.at[slot, d - 1, part(slot, i)],
                        s2.at[slot, i, d - 1], r2.at[slot, i, d - 1],
                        device_id={'cp': place * 8 + 2 * ((x + d) % 4) + c}, device_id_type=MESH).start()
    seqs = [lut(place, SEQ[slot]) for slot in range(2)]
    nths = [lut(place, NTH[slot]) for slot in range(2)]
    for i in reversed(range(PIECES)):
        for slot in range(2):
            @pl.when(i <= lims[slot])
            def _(i=i, slot=slot):
                for d in range(1, 4):
                    landed(xr.at[slot, d - 1, part(slot, i)], r2.at[slot, i, d - 1])
                zs[slot, part(slot, i)] = (own[slot, part(slot, i), x] + xr[slot, 0, part(slot, i)]
                                           + xr[slot, 1, part(slot, i)] + xr[slot, 2, part(slot, i)])
                for u in range(PP):
                    to = PP * i + u
                    send(zs.at[slot, to], home.at[seqs[slot], nths[slot]], s3.at[slot, to], r3.at[seqs[slot], nths[slot]],
                         to * 8 + 2 * x + c, me)
    cos = jnp.concatenate([cs[:, :64], cs[:, :64]], axis=1)
    sin = jnp.concatenate([-cs[:, 64:], cs[:, 64:]], axis=1)
    piece_me = place // PP
    for s in range(SEQS):
        for n, (chip, slot, last) in enumerate(CHIPS[s]):
            @pl.when(piece_me <= last)
            def _(s=s, n=n):
                landed(home.at[s, n], r3.at[s, n])

            @pl.when(piece_me > last)
            def _(s=s, n=n):
                home[s, n] = jnp.zeros((BLK, 2 * HEAD), F32)
        total = home[s, 0]
        for n in range(1, len(CHIPS[s])):
            total = total + home[s, n]
        dk = total[:, :HEAD] * SCALE
        other = jnp.concatenate([dk[:, 64:], dk[:, :64]], axis=1)
        gk[s] = (dk * cos - other * sin).astype(BF)
        gv[s] = total[:, HEAD:].astype(BF)
    for s in range(SEQS):
        landed(att.at[s], tr.at[s, 0])
        landed(gq.at[s], tr.at[s, 1])
    for k in range(6):
        g, tl = divmod(k, 2)
        j = lut(p, [META[n][g] for n in range(32)])
        src = j if tl == 0 else 31 - j

        @pl.when(src != p)
        def _(k=k):
            landed(o.at[k], ts.at[k, 0])
            landed(dq.at[k], ts.at[k, 1])
    for i in range(PIECES):
        for slot in range(2):
            @pl.when(i <= lims[slot])
            def _(i=i, slot=slot):
                landed(peer.at[slot, part(slot, i)], s1.at[slot, i])
                for d in range(1, 4):
                    landed(xr.at[slot, d - 1, part(slot, i)], s2.at[slot, i, d - 1])
                for u in range(PP):
                    to = PP * i + u

                    @pl.when(to != place)
                    def _(to=to):
                        landed(zs.at[slot, to], s3.at[slot, to])


def run_out(o, dq, dkv, cs):
    dma = pltpu.SemaphoreType.DMA
    any_ = pl.BlockSpec(memory_space=pl.ANY)
    vm = pl.BlockSpec(memory_space=pltpu.VMEM)
    v = pltpu.VMEM
    return pl.pallas_call(
        exchange_out,
        in_specs=[any_] * 3 + [vm], out_specs=[any_, any_, vm, vm],
        out_shape=[
            jax.ShapeDtypeStruct((6, ROWS, HEAD), BF), jax.ShapeDtypeStruct((6, ROWS, HEAD), BF),
            jax.ShapeDtypeStruct((6, BLK, HEAD), BF), jax.ShapeDtypeStruct((6, BLK, HEAD), BF)],
        scratch_shapes=[
            v((2, 16, 4, BLK, 2 * HEAD), F32), v((2, 16, 4, BLK, 2 * HEAD), F32), v((2, 3, 16, BLK, 2 * HEAD), F32),
            v((2, 16, BLK, 2 * HEAD), F32), v((SEQS, NCH, BLK, 2 * HEAD), F32),
            dma((2, PIECES)), dma((6, 2)), dma((6, 2)), dma((2, PIECES)), dma((2, PIECES)), dma((2, PIECES, 3)), dma((2, PIECES, 3)),
            dma((2, 16)), dma((SEQS, NCH))],
        compiler_params=pltpu.CompilerParams(has_side_effects=True, vmem_limit_bytes=63 << 20),
        name='exchange_out')(o, dq, dkv, cs)


def solution(mesh):
    query_spec = PS('dp', 'cp', None, None)
    kv_spec = PS('dp', 'cp', None)
    pos_spec = PS(('dp', 'cp'))

    def per_device(query, key, value, positions, grad_out):
        me = lax.axis_index('cp')
        inv_freq = jnp.power(jnp.float32(ROPE_BASE), -2.0 * jnp.arange(HEAD // 2, dtype=F32) / HEAD)
        angles = positions.astype(F32)[:, None] * inv_freq
        cos, sin = jnp.cos(angles), jnp.sin(angles)
        cs = jnp.concatenate([cos, sin], axis=1)
        k1, k2 = key[..., :64].astype(F32), key[..., 64:].astype(F32)
        kv = jnp.concatenate([(k1 * cos - k2 * sin).astype(BF), (k2 * cos + k1 * sin).astype(BF), value], axis=-1)
        place = me // 8
        row = lax.dynamic_index_in_dim(jnp.array(META, jnp.int32), 2 * place + me % 2, 0, keepdims=False)
        meta = row.at[7].set((me // 2) % 4)
        q, do, csr, kvr = run_in(query.reshape(6, ROWS, HEAD), grad_out.reshape(6, ROWS, HEAD), kv, cs)
        o, dq, dkv = run_attend(meta, q, do, csr, kvr.reshape(2, NC * CK, 2 * HEAD))
        att, gq, gk, gv = run_out(o, dq, dkv.reshape(2, 16, 4, 2, BLK, 2 * HEAD), cs)
        return att.reshape(query.shape), gq.reshape(query.shape), gk, gv

    return jax.shard_map(per_device, mesh=mesh, in_specs=(query_spec, kv_spec, kv_spec, pos_spec, query_spec),
                         out_specs=(query_spec, query_spec, kv_spec, kv_spec), check_vma=False)
```

time: 3410 us -> 157 us (0.05)
  the two profiles are of different devices: /device:TPU:96 before, /device:TPU:0 now
where the time goes in v1:
time: 157 us; the launch traced here: 156 us
  Pallas kernels  144 us (92%)
  local copies, waits for them, and re-layouts  7.86 us (5%)
  other arithmetic  4.01 us (3%)
    pallas_call x1, Pallas kernels, run_out(): pl.pallas_call(exchange_out, in_specs=[any_] * 3 + [vm], out_specs=[any_,...  66.8 us
    pallas_call x1, Pallas kernels, run_attend(): pl.pallas_call(attend, grid_spec=pltpu.PrefetchScalarGridSpec(num_scalar_...  41.2 us
    pallas_call x1, Pallas kernels, run_in(): pl.pallas_call(exchange_in, in_specs=[any_] * 4, out_specs=[any_] * 4, ou...  35.8 us
    unnamed x6, local copies, waits for them, and re-layouts  7.14 us

profile of v1, /device:TPU:0, one launch (start us, length us, event | category | flops | bytes accessed | tf_op | source)
XLA Modules:
  0.0 156.4 jit_solution(734844525389294759)
XLA Ops:
  0.7 0.7 dynamic-slice_bitcast_fusion
  1.4 0.0 copy-start
  1.4 0.7 convert_element_type.16
  2.1 0.1 multiply_cosine_fusion
  2.2 0.7 pad_maximum_fusion.1.cs
  2.9 1.0 fusion.1
  3.9 1.5 pad_maximum_fusion.kv
  5.4 35.8 %exchange_in.1 = (bf16[6,512,128]{2,1,0:T(8,128)(2,1)}, bf16[6,512,128]{2,1,0:T(8,128)(2,1)}, f32[6,32,128]{2,1,0:T(8,128)}, bf16[2,16,4,2,32,256]{5,4,3,2,1,0:T(8,128)(2,1)}) custom-call(bf16[6,512,128]{2,1,0:T(8,128)(2,1)} %bitcast.11, bf16[6,512,128]{2,1,0:T(8,128)(2,1)} %bitcast.12, bf16[6,32,256]{2,1,0:T(8,128)(2,1)} %pad_maximum_fusion.kv, ...), custom_call_target="tpu_custom_call" | custom-call | tf_op jit(solution)/shard_map/exchange_in/pallas_call | solution.py:174
  41.3 0.0 copy-done
  41.3 41.2 %attend.1 = (bf16[6,512,128]{2,1,0:T(8,128)(2,1)}, bf16[6,512,128]{2,1,0:T(8,128)(2,1)}, f32[2,4096,256]{2,1,0:T(8,128)}) custom-call(s32[10]{0:T(128)} %copy-done, bf16[6,512,128]{2,1,0:T(8,128)(2,1)} %get-tuple-element.27.q_ref, bf16[6,512,128]{2,1,0:T(8,128)(2,1)} %get-tuple-element.28.do_ref, f32[6,32,128]{2,1,0:T(8,128)} %get-tuple-element.29.cs_ref, ...), custom_call_target="tpu_custom_call" | custom-call | tf_op jit(solution)/shard_map/attend/pallas_call | solution.py:342
  82.5 66.8 %exchange_out.1 = (bf16[6,512,128]{2,1,0:T(8,128)(2,1)}, bf16[6,512,128]{2,1,0:T(8,128)(2,1)}, bf16[6,32,128]{2,1,0:T(8,128)(2,1)}, bf16[6,32,128]{2,1,0:T(8,128)(2,1)}) custom-call(bf16[6,512,128]{2,1,0:T(8,128)(2,1)} %get-tuple-element.31.o, bf16[6,512,128]{2,1,0:T(8,128)(2,1)} %get-tuple-element.32.dq, f32[2,16,4,2,32,256]{5,4,3,2,1,0:T(8,128)} %bitcast.9, ...), custom_call_target="tpu_custom_call" | custom-call | tf_op jit(solution)/shard_map/exchange_out/pallas_call | solution.py:460
  149.3 2.1 %copy.15 = bf16[6,32,16,128]{3,2,1,0:T(8,128)(2,1)} copy(bf16[6,32,16,128]{3,2,1,0:T(8,128)(2,1)} %bitcast.14) | data formatting | bytes 1572864
  151.4 2.1 %copy.16 = bf16[6,32,16,128]{3,2,1,0:T(8,128)(2,1)} copy(bf16[6,32,16,128]{3,2,1,0:T(8,128)(2,1)} %bitcast.13) | data formatting | bytes 1572864
  153.6 1.4 copy.17
  155.0 1.4 copy.18
  (2 shorter events, 0.0 us)
Async XLA Ops:
  1.4 39.9 %copy-start = (s32[10]{0:T(128)}, s32[10]{0:T(128)S(1)}, u32[]{:S(2)}) copy-start(s32[10]{0:T(128)S(1)} %constant_dynamic-update-slice_fusion.meta) | copy-start | bytes 124

commit v2 on v0

v2 whole, which is shorter than its diff:
```python
import jax
import jax.numpy as jnp
from jax import lax
from jax.experimental import pallas as pl
from jax.experimental.pallas import tpu as pltpu
from jax.sharding import PartitionSpec as PS

ROPE_BASE = 10000
SEQS, HEADS, HEAD, BLK = 6, 16, 128, 32
ROWS = BLK * HEADS
CK = 256
ENT = 24
SLOT1 = 12
SIDX = 56
SCALE = HEAD ** -0.5
C2 = SCALE * 1.4426950408889634
BIG = 1e30
BF, F32 = jnp.bfloat16, jnp.float32
MESH = pl.DeviceIdType.MESH

PLACE = [int(d, 16) for d in 'E45C2760D389FA1B']
ORDER = [[int(d, 16) for d in row] for row in (
    '530142768E9ADBCF',
    'CD8907162534BAFE',
    'F9E8A54BDC263701',
    'A52B34867901FDCE',
    'F9BAE538201746DC',
    'ABCD452130F867E9')]
PIECES = 4
PP = 16 // PIECES


def _tables():
    work = {}
    dest = [[0] * 16 for _ in range(SEQS)]
    limit = {}
    slots = {}
    for s in range(SEQS):
        for i, j in enumerate(ORDER[s]):
            q = 16 * (s % 3) + i
            f, g = divmod(q, 3)
            big_c = 8 * (s // 3) + f // 2
            slot = s % 3 - (6 * (f // 2)) // 16
            slots[big_c, s] = slot
            work[PLACE[big_c], f % 2, g] = (s, j, slot)
            dest[s][j] = PLACE[big_c] * 8 + (f % 2) * 4 + g
            limit[big_c, s] = max(limit.get((big_c, s), 0), ((31 - j) // 2) // PP)
    chips = [[(PLACE[c], slots[c, t], limit[c, t]) for (c, t) in sorted(slots) if t == s] for s in range(SEQS)]
    lim = [[-1] * 16, [-1] * 16]
    seq = [[0] * 16, [0] * 16]
    nth = [[0] * 16, [0] * 16]
    for s in range(SEQS):
        for n, (place, slot, last) in enumerate(chips[s]):
            lim[slot][place], seq[slot][place], nth[slot][place] = last, s, n
    meta = []
    for p in range(32):
        w = [work[p // 2, p % 2, g] for g in range(3)]
        meta.append([t[1] for t in w] + [t[2] for t in w] + [2 if lim[1][p // 2] >= 0 else 1] + [t[0] for t in w])
    return dest, chips, lim, seq, nth, meta


DEST, CHIPS, LIM, SEQ, NTH, META = _tables()
NCH = max(len(c) for c in CHIPS)


def lut(index, table):
    value = jnp.int32(table[0])
    for n in range(1, len(table)):
        if table[n] != table[n - 1]:
            value = jnp.where(index >= n, jnp.int32(table[n]), value)
    return value


def place_of():
    me = lax.axis_index('cp')
    return me, me % 2, (me // 2) % 4, me // 8


def send(src, dst, ssem, rsem, dev, me):
    @pl.when(dev != me)
    def _():
        pltpu.make_async_remote_copy(src, dst, ssem, rsem, device_id={'cp': dev}, device_id_type=MESH).start()

    @pl.when(dev == me)
    def _():
        pltpu.make_async_copy(src, dst, rsem).start()


def dot(a, b):
    return jnp.dot(a, b, preferred_element_type=F32)


def dot_nt(a, b):
    return lax.dot_general(a, b, (((1,), (1,)), ((), ())), preferred_element_type=F32)


def max8(v):
    return jnp.broadcast_to(jnp.max(v, axis=0, keepdims=True), (8, ROWS))


def sum8(v):
    return jnp.broadcast_to(jnp.sum(v, axis=0, keepdims=True), (8, ROWS))


def sub8(a, b):
    return a.reshape(-1, 8, ROWS) - b[None]


def turn(v, cs, sign):
    cos = jnp.concatenate([cs[:, :64], cs[:, :64]], axis=1)
    sin = jnp.concatenate([-cs[:, 64:], cs[:, 64:]], axis=1)
    v = v.reshape(BLK, HEADS, HEAD)
    other = jnp.concatenate([v[..., 64:], v[..., :64]], axis=-1)
    if sign > 0:
        out = v * cos[:, None, :] + other * sin[:, None, :]
    else:
        out = v * cos[:, None, :] - other * sin[:, None, :]
    return out.astype(BF).reshape(ROWS, HEAD)


def landed(ref, sem):
    pltpu.make_async_copy(ref, ref, sem).wait()


def sel(t, values):
    out = values[0]
    for k in range(1, len(values)):
        out = jnp.where(t == k, values[k], out)
    return out


def whole_step(q, do, kv, cs, att, gq, gk, gv,
               qraw, dor, csr, kvr, qn, qa, dot_t, hot, mk, kt, vt, sc, mx, mst, lst, dst, ot, dp_ref, osend, dqsend, csl,
               acc, peer, xr, zs, home,
               ks1, kr1, ks2, kr2, ks3, kr3, ts, tr, os_, or_, as1, ar1, as2, ar2, as3, ar3, cl):
    me, c, x, place = place_of()
    p = 2 * place + c
    jme = jnp.minimum(p, 31 - p)
    hi = p // 16
    lims = [lut(place, LIM[slot]) for slot in range(2)]
    seqs = [lut(place, SEQ[slot]) for slot in range(2)]
    nths = [lut(place, NTH[slot]) for slot in range(2)]
    piece_me = place // PP
    jg = [lut(p, [META[n][g] for n in range(32)]) for g in range(3)]
    slot_g = [lut(p, [META[n][3 + g] for n in range(32)]) for g in range(3)]
    seq_g = [lut(p, [META[n][7 + g] for n in range(32)]) for g in range(3)]
    pos = [v for g in range(3) for v in (jg[g], 31 - jg[g])]
    nch = [v // 2 + 1 for v in pos]
    par = [v % 2 for v in pos]
    ebase = [SLOT1 * slot_g[t // 2] for t in range(6)]
    partner = me + 1 - 2 * c

    def remote(src, dst, ssem, rsem, dev):
        return pltpu.make_async_remote_copy(src, dst, ssem, rsem, device_id={'cp': dev}, device_id_type=MESH)

    n = 0
    for s in range(SEQS):
        for (chip, slot, last) in CHIPS[s]:
            @pl.when(piece_me <= last)
            def _(s=s, chip=chip, slot=slot, n=n):
                send(kv.at[s], kvr.at[SLOT1 * slot + place, x, c], ks1.at[n], kr1.at[slot, piece_me], chip * 8 + 2 * x + c, me)
            n += 1
    for a in range(3):
        here, there = ((q, qraw), (cs, csr), (do, dor))[a]
        for s in range(SEQS):
            code = lut(jme, DEST[s])
            k = 2 * (code % 4) + hi
            dev = (code // 8) * 8 + 2 * x + (code // 4) % 2
            send(cs if a == 1 else here.at[s], there.at[k], ts.at[s, a], tr.at[k, a], dev, me)
    pltpu.make_async_copy(cs, csl, cl).start()

    @pl.loop(0, ENT)
    def _(e):
        acc[e] = jnp.zeros((4, 2, BLK, 2 * HEAD), F32)
    row = lax.broadcasted_iota(jnp.int32, (HEAD, ROWS), 0)
    col = lax.broadcasted_iota(jnp.int32, (HEAD, ROWS), 1)
    hot[...] = jnp.where(col // HEADS == row, 1.0, 0.0).astype(BF)
    ki = lax.broadcasted_iota(jnp.int32, (CK, HEAD), 0)
    di = lax.broadcasted_iota(jnp.int32, (CK, HEAD), 1)
    mk[0] = jnp.zeros((CK, HEAD), BF)
    for cc in range(2):
        mk[1 + cc] = jnp.where((di < BLK) & (ki > di + 64 * x + BLK * cc), -BIG, 0.0).astype(BF)

    @pl.loop(0, 6)
    def _(t):
        ot[t] = jnp.zeros((HEAD, ROWS), F32)
        mst[t] = jnp.full((8, ROWS), -BIG, F32)
        lst[t] = jnp.zeros((8, ROWS), F32)

    def ents(slot, i):
        return pl.ds(SLOT1 * slot + PP * i, PP)

    def relay_x(i):
        for slot in range(2):
            @pl.when(i <= lims[slot])
            def _(slot=slot):
                mine = kvr.at[ents(slot, i), x, c]
                landed(mine, kr1.at[slot, i])
                for d in range(1, 4):
                    remote(mine, mine, ks2.at[slot, i, d - 1], kr2.at[slot, i, d - 1], place * 8 + 2 * ((x + d) % 4) + c).start()

    def relay_core(i):
        for slot in range(2):
            @pl.when(i <= lims[slot])
            def _(slot=slot):
                for d in range(1, 4):
                    landed(kvr.at[ents(slot, i), (x + 4 - d) % 4, c], kr2.at[slot, i, d - 1])
                both = kvr.at[ents(slot, i), :, c]
                remote(both, both, ks3.at[slot, i], kr3.at[slot, i], partner).start()

    @pl.loop(0, PIECES)
    def _(i):
        relay_x(i)
    relay_core(0)

    @pl.loop(0, 6)
    def _(t):
        landed(qraw.at[t], tr.at[t, 0])
        landed(csr.at[t], tr.at[t, 1])
        rq = turn(qraw[t].astype(F32), csr[t], 1)
        qn[t] = rq
        qa[t] = rq.T

    def phase(pc):
        cum = [jnp.int32(0)]
        for t in range(6):
            cum.append(cum[-1] + jnp.minimum(jnp.maximum(nch[t] - PP * pc, 0), PP))

        def dec(i):
            t = jnp.int32(0)
            for k in range(1, 6):
                t = t + (i >= cum[k]).astype(jnp.int32)
            ch = PP * pc + i - sel(t, cum[:6])
            return t, ch, sel(t, ebase) + ch
        return cum[6], dec

    def run(count, pair, last):
        quads = (count - 1) // 4

        @pl.loop(0, quads)
        def _(b):
            for u in range(4):
                pair(4 * b + u, 4 * b, u)
        rest = (count - 1) % 4
        for r in range(4):
            @pl.when(rest == r)
            def _(r=r):
                for u in range(r):
                    pair(4 * quads + u, 4 * quads, u)
                last(4 * quads + r, 4 * quads, r)

    def keys(e):
        return kvr[e, :, :, :, :HEAD].reshape(CK, HEAD)

    def values(e):
        return kvr[e, :, :, :, HEAD:].reshape(CK, HEAD)

    base = [jnp.int32(0)]
    for pc in range(PIECES):
        base.append(base[-1] + phase(pc)[0])

    @pl.loop(0, PIECES)
    def _(pc):
        @pl.when(pc < PIECES - 1)
        def _():
            relay_core(pc + 1)
        for slot in range(2):
            @pl.when(pc <= lims[slot])
            def _(slot=slot):
                landed(kvr.at[ents(slot, pc), :, 1 - c], kr3.at[slot, pc])

                @pl.loop(0, PP)
                def _(v):
                    e = SLOT1 * slot + PP * pc + v
                    kt[e] = keys(e).T
                    vt[e] = values(e).T
        count, dec = phase(pc)
        start = sel(pc, base[:PIECES])

        def s_step(i, sb, u):
            t, ch, e = dec(i)
            mask = jnp.where(ch == sel(t, nch) - 1, 1 + sel(t, par), 0)
            ka = jnp.concatenate([keys(e), mk[mask]], axis=1)
            qh = jnp.concatenate([qa[t], hot[...]], axis=0)
            sv = dot(ka, qh) * C2
            sc.at[pl.ds(sb, 5)][u] = sv
            mx.at[pl.ds(sb, 5)][u] = jnp.max(sv.reshape(CK // 8, 8, ROWS), axis=0)

        def o_step(i, sb, u):
            t, ch, e = dec(i)
            mo = mst[t]
            mn = jnp.maximum(mo, max8(mx.at[pl.ds(sb, 5)][u]))
            al = jnp.exp2(mo - mn)
            ev = jnp.exp2(sub8(sc.at[pl.ds(sb, 5)][u], mn))
            mst[t] = mn
            lst[t] = lst[t] * al + jnp.sum(ev, axis=0)
            ot[t] = (ot[t].reshape(-1, 8, ROWS) * al[None]).reshape(HEAD, ROWS) + dot(vt[e], ev.reshape(CK, ROWS).astype(BF))

        def pair(i, b, u):
            s_step(i + 1, start + b, u + 1)
            o_step(i, start + b, u)

        @pl.when(count > 0)
        def _():
            s_step(jnp.int32(0), start, 0)
            run(count, pair, lambda i, b, u: o_step(i, start + b, u))

    for t in range(6):
        landed(dor.at[t], tr.at[t, 2])
        dot_t[t] = dor[t].T
        l = sum8(lst[t])
        o = (ot[t].reshape(-1, 8, ROWS) / l[None]).reshape(HEAD, ROWS).astype(BF)
        osend[t] = o.T
        dev = (pos[t] // 2) * 8 + 2 * x + par[t]
        send(osend.at[t], att.at[seq_g[t // 2]], os_.at[t, 0], or_.at[seq_g[t // 2], 0], dev, me)
        dst[t] = sum8(jnp.sum((o.astype(F32) * dot_t[t].astype(F32)).reshape(-1, 8, ROWS), axis=0))
        mst[t] = mst[t] + jnp.log2(l)
        ot[t] = jnp.zeros((HEAD, ROWS), F32)

    def sum_core(i):
        for slot in range(2):
            @pl.when(i <= lims[slot])
            def _(slot=slot):
                remote(acc.at[ents(slot, i), :, 1 - c], peer.at[ents(slot, i)], as1.at[slot, i], ar1.at[slot, i], partner).start()

    def sum_x(i):
        for slot in range(2):
            @pl.when(i <= lims[slot])
            def _(slot=slot):
                landed(peer.at[ents(slot, i)], ar1.at[slot, i])

                @pl.loop(0, PP)
                def _(v):
                    e = SLOT1 * slot + PP * i + v
                    acc[e, :, c] += peer[e]
                for d in range(1, 4):
                    remote(acc.at[ents(slot, i), (x + d) % 4, c], xr.at[d - 1, ents(slot, i)],
                           as2.at[slot, i, d - 1], ar2.at[slot, i, d - 1], place * 8 + 2 * ((x + d) % 4) + c).start()

    def sum_home(i):
        for slot in range(2):
            @pl.when(i <= lims[slot])
            def _(slot=slot):
                for d in range(1, 4):
                    landed(xr.at[d - 1, ents(slot, i)], ar2.at[slot, i, d - 1])
                for v in range(PP):
                    to = PP * i + v
                    e = SLOT1 * slot + to
                    zs[e] = acc[e, x, c] + xr[0, e] + xr[1, e] + xr[2, e]
                    send(zs.at[e], home.at[seqs[slot], nths[slot]], as3.at[e], ar3.at[seqs[slot], nths[slot]],
                         to * 8 + 2 * x + c, me)

    @pl.loop(0, PIECES)
    def _(back):
        pc = PIECES - 1 - back
        count, dec = phase(pc)
        start = sel(pc, base[:PIECES])

        def d_step(i, u):
            t, ch, e = dec(i)
            dp_ref[u % 4] = dot(values(e), dot_t[t])

        def g_step(i, sb, u, ahead):
            t, ch, e = dec(i)
            pr = jnp.exp2(sub8(sc.at[pl.ds(sb, 5)][u], mst[t]))
            prb = pr.reshape(CK, ROWS).astype(BF)
            acc[e, :, :, :, HEAD:] += dot(prb, dor[t]).reshape(4, 2, BLK, HEAD)
            ahead()
            ds = (pr * sub8(dp_ref[u % 4], dst[t])).reshape(CK, ROWS).astype(BF)
            ot[t] += dot(kt[e], ds)
            acc[e, :, :, :, :HEAD] += dot(ds, qn[t]).reshape(4, 2, BLK, HEAD)

        @pl.when(count > 0)
        def _():
            d_step(jnp.int32(0), 0)
            run(count, lambda i, b, u: g_step(i, start + b, u, lambda: d_step(i + 1, u + 1)),
                lambda i, b, u: g_step(i, start + b, u, lambda: None))
        sum_core(pc)

        @pl.when(back >= 1)
        def _():
            sum_x(pc + 1)

        @pl.when(back >= 2)
        def _():
            sum_home(pc + 2)

    for t in range(6):
        dqsend[t] = turn((ot[t] * SCALE).T, csr[t], -1)
        dev = (pos[t] // 2) * 8 + 2 * x + par[t]
        send(dqsend.at[t], gq.at[seq_g[t // 2]], os_.at[t, 1], or_.at[seq_g[t // 2], 1], dev, me)
    sum_x(0)
    sum_home(1)
    sum_home(0)

    pltpu.make_async_copy(cs, csl, cl).wait()
    tab = csl[...]
    cos = jnp.concatenate([tab[:, :64], tab[:, :64]], axis=1)
    sin = jnp.concatenate([-tab[:, 64:], tab[:, 64:]], axis=1)
    for s in range(SEQS):
        for m, (chip, slot, last) in enumerate(CHIPS[s]):
            @pl.when(piece_me <= last)
            def _(s=s, m=m):
                landed(home.at[s, m], ar3.at[s, m])

            @pl.when(piece_me > last)
            def _(s=s, m=m):
                home[s, m] = jnp.zeros((BLK, 2 * HEAD), F32)
        total = home[s, 0]
        for m in range(1, len(CHIPS[s])):
            total = total + home[s, m]
        dk = total[:, :HEAD] * SCALE
        other = jnp.concatenate([dk[:, 64:], dk[:, :64]], axis=1)
        gk[s] = (dk * cos - other * sin).astype(BF)
        gv[s] = total[:, HEAD:].astype(BF)

    for s in range(SEQS):
        landed(att.at[s], or_.at[s, 0])
        landed(gq.at[s], or_.at[s, 1])
    n = 0
    for s in range(SEQS):
        for (chip, slot, last) in CHIPS[s]:
            @pl.when((piece_me <= last) & (place != chip))
            def _(s=s, n=n):
                landed(kv.at[s], ks1.at[n])
            n += 1
    for s in range(SEQS):
        code = lut(jme, DEST[s])
        dev = (code // 8) * 8 + 2 * x + (code // 4) % 2

        @pl.when(dev != me)
        def _(s=s):
            landed(q.at[s], ts.at[s, 0])
            landed(cs, ts.at[s, 1])
            landed(do.at[s], ts.at[s, 2])
    for t in range(6):
        @pl.when(pos[t] != p)
        def _(t=t):
            landed(osend.at[t], os_.at[t, 0])
            landed(dqsend.at[t], os_.at[t, 1])
    for slot in range(2):
        @pl.loop(0, lims[slot] + 1)
        def _(i, slot=slot):
            for d in range(1, 4):
                landed(kvr.at[ents(slot, i), x, c], ks2.at[slot, i, d - 1])
                landed(xr.at[d - 1, ents(slot, i)], as2.at[slot, i, d - 1])
            landed(kvr.at[ents(slot, i), :, c], ks3.at[slot, i])
            landed(peer.at[ents(slot, i)], as1.at[slot, i])
            for v in range(PP):
                to = PP * i + v

                @pl.when(to != place)
                def _(to=to):
                    landed(zs.at[SLOT1 * slot + to], as3.at[SLOT1 * slot + to])


def run_whole(q, do, kv, cs):
    dma = pltpu.SemaphoreType.DMA
    n_kv = sum(len(c) for c in CHIPS)
    any_ = pl.BlockSpec(memory_space=pl.ANY)
    vm = pl.BlockSpec(memory_space=pltpu.VMEM)
    v = pltpu.VMEM
    two = 2 * HEAD
    return pl.pallas_call(
        whole_step,
        in_specs=[any_] * 4, out_specs=[any_, any_, vm, vm],
        out_shape=[
            jax.ShapeDtypeStruct((6, ROWS, HEAD), BF), jax.ShapeDtypeStruct((6, ROWS, HEAD), BF),
            jax.ShapeDtypeStruct((6, BLK, HEAD), BF), jax.ShapeDtypeStruct((6, BLK, HEAD), BF)],
        scratch_shapes=[
            v((6, ROWS, HEAD), BF), v((6, ROWS, HEAD), BF), v((6, BLK, HEAD), F32), v((ENT, 4, 2, BLK, two), BF),
            v((6, ROWS, HEAD), BF), v((6, HEAD, ROWS), BF), v((6, HEAD, ROWS), BF), v((HEAD, ROWS), BF), v((3, CK, HEAD), BF),
            v((ENT, HEAD, CK), BF), v((ENT, HEAD, CK), BF),
            v((SIDX, CK, ROWS), F32), v((SIDX, 8, ROWS), F32), v((6, 8, ROWS), F32), v((6, 8, ROWS), F32), v((6, 8, ROWS), F32),
            v((6, HEAD, ROWS), F32), v((4, CK, ROWS), F32), v((6, ROWS, HEAD), BF), v((6, ROWS, HEAD), BF), v((BLK, HEAD), F32),
            v((ENT, 4, 2, BLK, two), F32), v((ENT, 4, BLK, two), F32), v((3, ENT, BLK, two), F32), v((ENT, BLK, two), F32),
            v((SEQS, NCH, BLK, two), F32),
            dma((n_kv,)), dma((2, PIECES)), dma((2, PIECES, 3)), dma((2, PIECES, 3)), dma((2, PIECES)), dma((2, PIECES)),
            dma((6, 3)), dma((6, 3)), dma((6, 2)), dma((6, 2)),
            dma((2, PIECES)), dma((2, PIECES)), dma((2, PIECES, 3)), dma((2, PIECES, 3)), dma((ENT,)), dma((SEQS, NCH)), dma(())],
        compiler_params=pltpu.CompilerParams(has_side_effects=True, vmem_limit_bytes=67043328),
        name='whole_step')(q, do, kv, cs)


def solution(mesh):
    query_spec = PS('dp', 'cp', None, None)
    kv_spec = PS('dp', 'cp', None)
    pos_spec = PS(('dp', 'cp'))

    def per_device(query, key, value, positions, grad_out):
        inv_freq = jnp.power(jnp.float32(ROPE_BASE), -2.0 * jnp.arange(HEAD // 2, dtype=F32) / HEAD)
        angles = positions.astype(F32)[:, None] * inv_freq
        cos, sin = jnp.cos(angles), jnp.sin(angles)
        cs = jnp.concatenate([cos, sin], axis=1)
        k1, k2 = key[..., :64].astype(F32), key[..., 64:].astype(F32)
        kv = jnp.concatenate([(k1 * cos - k2 * sin).astype(BF), (k2 * cos + k1 * sin).astype(BF), value], axis=-1)
        att, gq, gk, gv = run_whole(query.reshape(6, ROWS, HEAD), grad_out.reshape(6, ROWS, HEAD), kv, cs)
        return att.reshape(query.shape), gq.reshape(query.shape), gk, gv

    return jax.shard_map(per_device, mesh=mesh, in_specs=(query_spec, kv_spec, kv_spec, pos_spec, query_spec),
                         out_specs=(query_spec, query_spec, kv_spec, kv_spec), check_vma=False)
```

time: 3410 us -> 111 us (0.03)
  the two profiles are of different devices: /device:TPU:96 before, /device:TPU:0 now
where the time goes in v2:
time: 111 us; the launch traced here: 110 us
  Pallas kernels  102 us (92%)
  local copies, waits for them, and re-layouts  5.24 us (5%)
  other arithmetic  2.35 us (2%)
    pallas_call x1, Pallas kernels, run_whole(): pl.pallas_call(whole_step, in_specs=[any_] * 4, out_specs=[any_, any_, vm...  102 us
    unnamed x14, local copies, waits for them, and re-layouts  5.24 us

profile of v2, /device:TPU:0, one launch (start us, length us, event | category | flops | bytes accessed | tf_op | source)
XLA Modules:
  0.0 110.4 jit_solution(14420462422416680769)
XLA Ops:
  0.6 0.0 copy-start.1
  0.6 0.7 convert_element_type.16
  1.3 0.1 multiply_cosine_fusion
  1.5 0.7 pad_maximum_fusion.1.cs
  2.2 0.0 copy-done.1
  2.2 0.0 copy-start.4
  2.2 0.1 fusion.1
  2.3 0.7 copy-done.4
  3.0 0.7 pad_maximum_fusion.kv
  3.7 102.2 %whole_step.1 = (bf16[6,512,128]{2,1,0:T(8,128)(2,1)}, bf16[6,512,128]{2,1,0:T(8,128)(2,1)}, bf16[6,32,128]{2,1,0:T(8,128)(2,1)}, bf16[6,32,128]{2,1,0:T(8,128)(2,1)}) custom-call(bf16[6,512,128]{2,1,0:T(8,128)(2,1)} %bitcast.4, bf16[6,512,128]{2,1,0:T(8,128)(2,1)} %bitcast.5, bf16[6,32,256]{2,1,0:T(8,128)(2,1)} %pad_maximum_fusion.kv, ...), custom_call_target="tpu_custom_call" | custom-call | tf_op jit(solution)/shard_map/whole_step/pallas_call | solution.py:464
  105.9 0.0 copy-start
  105.9 2.2 %copy.13 = bf16[6,32,16,128]{3,2,1,0:T(8,128)(2,1)} copy(bf16[6,32,16,128]{3,2,1,0:T(8,128)(2,1)} %bitcast.7) | data formatting | bytes 1572864
  108.1 0.0 copy-done
  108.1 0.0 copy-start.3
  108.1 0.9 copy.14
  109.0 0.0 copy-done.3
  109.0 0.0 copy-start.2
  109.0 0.6 copy.15
  109.6 0.2 copy-done.2
  109.8 0.6 copy.16
  (1 shorter events, 0.0 us)
Async XLA Ops:
  0.6 1.5 %copy-start.1 = (bf16[6,32,128]{2,1,0:T(8,128)(2,1)S(1)}, bf16[6,32,128]{2,1,0:T(8,128)(2,1)}, u32[]{:S(2)}) copy-start(bf16[6,32,128]{2,1,0:T(8,128)(2,1)} %param.6) | copy-start | bytes 147460
  2.2 0.8 copy-start.4
  105.9 2.2 %copy-start = (bf16[6,512,128]{2,1,0:T(8,128)(2,1)S(1)}, bf16[6,512,128]{2,1,0:T(8,128)(2,1)}, u32[]{:S(2)}) copy-start(bf16[6,512,128]{2,1,0:T(8,128)(2,1)} %get-tuple-element.9) | copy-start | bytes 2359300
  108.1 0.9 copy-start.3
  109.0 0.8 copy-start.2

commit v3 on v2

v3 whole, which is shorter than its diff:
```python
import jax
import jax.numpy as jnp
from jax import lax
from jax.experimental import pallas as pl
from jax.experimental.pallas import tpu as pltpu
from jax.sharding import PartitionSpec as PS

ROPE_BASE = 10000
SEQS, HEADS, HEAD, BLK = 6, 16, 128, 32
ROWS = BLK * HEADS
CK = 256
ENT = 24
SLOT1 = 12
SIDX = 55
SCALE = HEAD ** -0.5
C2 = SCALE * 1.4426950408889634
BIG = 1e30
HH, TWO = HEAD // 2, 2 * HEAD
BF, F32 = jnp.bfloat16, jnp.float32
MESH = pl.DeviceIdType.MESH

PLACE = [int(d, 16) for d in 'E47B1560328CDA9F']
ORDER = [[int(d, 16) for d in row] for row in (
    '5304218A67B9FDCE',
    'EF69BA87215304DC',
    'CEFDBA5498037126',
    '169078BA4325DCFE',
    'FE167980B53A42CD',
    'CDFEB5894A173260')]
PIECES = 4
PP = 16 // PIECES
HALF = PP // 2
HALVES = 16 // HALF


def _tables():
    work = {}
    dest = [[0] * 16 for _ in range(SEQS)]
    limit = {}
    slots = {}
    for s in range(SEQS):
        for i, j in enumerate(ORDER[s]):
            q = 16 * (s % 3) + i
            f, core, g = q // 6, q % 2, q % 6 // 2
            big_c = 8 * (s // 3) + f
            slot = s % 3 - (6 * f) // 16
            slots[big_c, s] = slot
            work[PLACE[big_c], core, g] = (s, j, slot)
            dest[s][j] = PLACE[big_c] * 8 + core * 4 + g
            limit[big_c, s] = max(limit.get((big_c, s), 0), ((31 - j) // 2) // HALF)
    chips = [[(PLACE[c], slots[c, t], limit[c, t]) for (c, t) in sorted(slots) if t == s] for s in range(SEQS)]
    lim = [[-1] * 16, [-1] * 16]
    seq = [[0] * 16, [0] * 16]
    nth = [[0] * 16, [0] * 16]
    for s in range(SEQS):
        for n, (place, slot, last) in enumerate(chips[s]):
            lim[slot][place], seq[slot][place], nth[slot][place] = last, s, n
    meta = []
    for p in range(32):
        w = [work[p // 2, p % 2, g] for g in range(3)]
        meta.append([t[1] for t in w] + [t[2] for t in w] + [2 if lim[1][p // 2] >= 0 else 1] + [t[0] for t in w])
    return dest, chips, lim, seq, nth, meta


DEST, CHIPS, LIM, SEQ, NTH, META = _tables()
NCH = max(len(c) for c in CHIPS)


def lut(index, table):
    value = jnp.int32(table[0])
    for n in range(1, len(table)):
        if table[n] != table[n - 1]:
            value = jnp.where(index >= n, jnp.int32(table[n]), value)
    return value


def device(place, x, core):
    return place * 8 + 2 * x + core


def place_of():
    me = lax.axis_index('cp')
    return me, me % 2, (me // 2) % 4, me // 8


def send(src, dst, ssem, rsem, dev, me):
    @pl.when(dev != me)
    def _():
        pltpu.make_async_remote_copy(src, dst, ssem, rsem, device_id={'cp': dev}, device_id_type=MESH).start()

    @pl.when(dev == me)
    def _():
        pltpu.make_async_copy(src, dst, rsem).start()


def dot(a, b):
    return jnp.dot(a, b, preferred_element_type=F32)


def dot_nt(a, b):
    return lax.dot_general(a, b, (((1,), (1,)), ((), ())), preferred_element_type=F32)


def max8(v):
    return jnp.broadcast_to(jnp.max(v, axis=0, keepdims=True), (8, ROWS))


def sum8(v):
    return jnp.broadcast_to(jnp.sum(v, axis=0, keepdims=True), (8, ROWS))


def sub8(a, b):
    return a.reshape(-1, 8, ROWS) - b[None]


def turn(v, cs, sign):
    cos = jnp.concatenate([cs[:, :HH], cs[:, :HH]], axis=1)
    sin = jnp.concatenate([-cs[:, HH:], cs[:, HH:]], axis=1)
    v = v.reshape(BLK, HEADS, HEAD)
    other = jnp.concatenate([v[..., HH:], v[..., :HH]], axis=-1)
    if sign > 0:
        out = v * cos[:, None, :] + other * sin[:, None, :]
    else:
        out = v * cos[:, None, :] - other * sin[:, None, :]
    return out.astype(BF).reshape(ROWS, HEAD)


def landed(ref, sem):
    pltpu.make_async_copy(ref, ref, sem).wait()


def sel(t, values):
    out = values[0] + jnp.int32(0)
    for k in range(1, len(values)):
        out = jnp.where(t == k, values[k], out)
    return out


def whole_step(q, do, key, value, pos32, freq, att, gq, gk, gv,
               qraw, dor, csr, kvr, qn, qa, dot_t, hot, mk, kt, vt, sc, mx, mst, lst, dst, ot, dp_ref, csl,
               acc, peer, xr, zs, home, keyl, kv, posl,
               ks1, kr1, ks2, kr2, ks3, kr3, ts, tr, os_, or_, as1, ar1, as2, ar2, as3, ar3, cl, kl):
    me, c, x, place = place_of()
    p = 2 * place + c
    jme = jnp.minimum(p, 31 - p)
    hi = p // 16
    lims = [lut(place, LIM[slot]) for slot in range(2)]
    seqs = [lut(place, SEQ[slot]) for slot in range(2)]
    nths = [lut(place, NTH[slot]) for slot in range(2)]
    half_me = place // HALF
    jg = [lut(p, [META[n][g] for n in range(len(META))]) for g in range(3)]
    slot_g = [lut(p, [META[n][3 + g] for n in range(len(META))]) for g in range(3)]
    seq_g = [lut(p, [META[n][7 + g] for n in range(len(META))]) for g in range(3)]
    pos = [v for g in range(3) for v in (jg[g], 31 - jg[g])]
    nch = [v // 2 + 1 for v in pos]
    par = [v % 2 for v in pos]
    ebase = [SLOT1 * slot_g[t // 2] for t in range(6)]
    partner = me + 1 - 2 * c

    def remote(src, dst, ssem, rsem, dev):
        return pltpu.make_async_remote_copy(src, dst, ssem, rsem, device_id={'cp': dev}, device_id_type=MESH)

    fetch = [pltpu.make_async_copy(pos32, posl, cl), pltpu.make_async_copy(key, keyl, kl.at[0]),
             pltpu.make_async_copy(value, kv.at[:, :, HEAD:], kl.at[1])]
    for copy in fetch:
        copy.start()
    barrier = pltpu.get_barrier_semaphore()

    def greet(dev):
        pl.semaphore_signal(barrier, inc=1, device_id={'cp': dev}, device_id_type=MESH)

    @pl.loop(0, 16)
    def _(other):
        greet(device(other, x, 1 - c))

        @pl.when(other != place)
        def _():
            greet(device(other, x, c))
    for d in range(1, 4):
        greet(device(place, (x + d) % 4, c))
    for copy in fetch:
        copy.wait()
    inv = freq[...]
    for t in range(BLK):
        csl[t:t + 1, :HH] = posl[t].astype(F32) * inv
    ang = csl[:, :HH]
    csl[:, :HH] = jnp.cos(ang)
    csl[:, HH:] = jnp.sin(ang)
    tab = csl[...]
    cos = jnp.concatenate([tab[:, :HH], tab[:, :HH]], axis=1)
    sin = jnp.concatenate([-tab[:, HH:], tab[:, HH:]], axis=1)
    for s in range(SEQS):
        kf = keyl[s].astype(F32)
        kv[s, :, :HEAD] = (kf * cos + jnp.concatenate([kf[:, HH:], kf[:, :HH]], axis=1) * sin).astype(BF)
    pl.semaphore_wait(barrier, 34)

    def work_of(s):
        code = lut(jme, DEST[s])
        return code % 4, 2 * (code % 4) + hi, device(code // 8, x, (code // 4) % 2)

    def send_q():
        for g in range(3):
            for s in range(SEQS):
                when, k, dev = work_of(s)

                @pl.when(when == g)
                def _(s=s, k=k, dev=dev):
                    send(q.at[s], qraw.at[k], ts.at[s, 0], tr.at[k, 0], dev, me)
                    send(csl, csr.at[k], ts.at[s, 1], tr.at[k, 1], dev, me)

    def send_do():
        for s in range(SEQS):
            _, k, dev = work_of(s)
            send(do.at[s], dor.at[k], ts.at[s, 2], tr.at[k, 2], dev, me)

    n = 0
    for s in range(SEQS):
        for (chip, slot, last) in CHIPS[s]:
            @pl.when(half_me <= last)
            def _(s=s, chip=chip, slot=slot, n=n):
                send(kv.at[s], kvr.at[SLOT1 * slot + place, x, c], ks1.at[n], kr1.at[slot, half_me], device(chip, x, c), me)
            n += 1

    @pl.loop(0, ENT)
    def _(e):
        acc[e] = jnp.zeros((4, 2, BLK, TWO), F32)
    row = lax.broadcasted_iota(jnp.int32, (HEAD, ROWS), 0)
    col = lax.broadcasted_iota(jnp.int32, (HEAD, ROWS), 1)
    hot[...] = jnp.where(col // HEADS == row, 1.0, 0.0).astype(BF)
    ki = lax.broadcasted_iota(jnp.int32, (CK, HEAD), 0)
    di = lax.broadcasted_iota(jnp.int32, (CK, HEAD), 1)
    mk[0] = jnp.zeros((CK, HEAD), BF)
    for cc in range(2):
        mk[1 + cc] = jnp.where((di < BLK) & (ki > di + 64 * x + BLK * cc), -BIG, 0.0).astype(BF)

    @pl.loop(0, 6)
    def _(t):
        ot[t] = jnp.zeros((HEAD, ROWS), F32)
        mst[t] = jnp.full((8, ROWS), -BIG, F32)
        lst[t] = jnp.zeros((8, ROWS), F32)

    right = device(place, (x + 1) % 4, c)
    left = device(place, (x + 3) % 4, c)

    def halves(i):
        return [u for h in range(2) for u in half(i, h)]

    def half(i, h):
        slots = 1 if isinstance(i, int) and i == PIECES - 1 else 2
        return [(slot, h, 2 * i + h) for slot in range(slots)]

    def ents(slot, n):
        return pl.ds(SLOT1 * slot + HALF * n, HALF)

    def relay_x(i):
        for slot, h, n in halves(i):
            @pl.when(n <= lims[slot])
            def _(slot=slot, n=n):
                mine = kvr.at[ents(slot, n), x, c]
                landed(mine, kr1.at[slot, n])
                remote(mine, mine, ks2.at[slot, n, 0], kr2.at[slot, n, 0], right).start()
                remote(mine, mine, ks2.at[slot, n, 1], kr2.at[slot, n, 1], left).start()

    def relay_x2(i):
        for slot, h, n in halves(i):
            @pl.when(n <= lims[slot])
            def _(slot=slot, h=h, n=n):
                theirs = kvr.at[ents(slot, n), (x + 3 - 2 * h) % 4, c]
                landed(theirs, kr2.at[slot, n, h])
                remote(theirs, theirs, ks2.at[slot, n, 2], kr2.at[slot, n, 2], left if h else right).start()

    def relay_core(i):
        for slot, h, n in halves(i):
            @pl.when(n <= lims[slot])
            def _(slot=slot, h=h, n=n):
                landed(kvr.at[ents(slot, n), x, c], kr2.at[slot, n, 1 - h])
                landed(kvr.at[ents(slot, n), x, c], kr2.at[slot, n, 2])
                both = kvr.at[ents(slot, n), :, c]
                remote(both, both, ks3.at[slot, n], kr3.at[slot, n], partner).start()

    relay_x(0)
    relay_x(1)
    send_q()
    relay_x(2)
    relay_x(3)
    relay_x2(0)
    relay_x2(1)
    relay_core(0)

    def prep_q(t):
        landed(qraw.at[t], tr.at[t, 0])
        landed(csr.at[t], tr.at[t, 1])
        rq = turn(qraw[t].astype(F32), csr[t], 1)
        qn[t] = rq
        qa[t] = rq.T

    def phase(pc):
        cum = [jnp.int32(0)]
        for t in range(6):
            cum.append(cum[-1] + jnp.minimum(jnp.maximum(nch[t] - PP * pc, 0), PP))
        return cum

    base = [jnp.int32(0)]
    for pc in range(PIECES):
        base.append(base[-1] + phase(pc)[6])

    def segment(k):
        pc = jnp.maximum(k - 2, 0)
        cum = phase(pc)
        part = jnp.minimum(k, 3)
        first = sel(part, [cum[0], cum[2], cum[4], cum[0]])
        count = sel(part, [cum[2], cum[4], cum[6], cum[6]]) - first

        def dec(i):
            i = i + first
            t = jnp.int32(0)
            for n in range(1, 6):
                t = t + (i >= cum[n]).astype(jnp.int32)
            ch = PP * pc + i - sel(t, cum[:6])
            return t, ch, sel(t, ebase) + ch
        return pc, sel(pc, base[:PIECES]) + first, count, dec

    def run(count, pair, last, between=None):
        quads = (count - 1) // 4

        def quad(b):
            for u in range(4):
                pair(4 * b + u, 4 * b, u)
        if between is None:
            pl.loop(0, quads)(quad)
        else:
            @pl.loop(0, quads)
            def _(b):
                @pl.when(b == 2)
                def _():
                    between()
                quad(b)

            @pl.when(quads <= 2)
            def _():
                between()
        rest = (count - 1) % 4
        for r in range(4):
            @pl.when(rest == r)
            def _(r=r):
                for u in range(r):
                    pair(4 * quads + u, 4 * quads, u)
                last(4 * quads + r, 4 * quads, r)

    def keys(e):
        return kvr[e, :, :, :, :HEAD].reshape(CK, HEAD)

    def values(e):
        return kvr[e, :, :, :, HEAD:].reshape(CK, HEAD)

    @pl.loop(0, 6)
    def _(k):
        @pl.when((k >= 1) & (k <= 3))
        def _():
            relay_core(k)
        @pl.when(k < 3)
        def _():
            prep_q(2 * k)
            prep_q(2 * k + 1)
        @pl.when(k == 0)
        def _():
            send_do()
            relay_x2(2)
            relay_x2(3)
        pc, start, count, dec = segment(k)
        for slot, h, n in halves(pc):
            @pl.when((n <= lims[slot]) & ((k == 0) | (k > 2)))
            def _(slot=slot, n=n):
                landed(kvr.at[ents(slot, n), :, 1 - c], kr3.at[slot, n])
                for v in range(HALF):
                    e = SLOT1 * slot + HALF * n + v
                    kt[e] = keys(e).T
                    vt[e] = values(e).T

        def s_step(i, sb, u):
            t, ch, e = dec(i)
            mask = jnp.where(ch == sel(t, nch) - 1, 1 + sel(t, par), 0)
            ka = jnp.concatenate([keys(e), mk[mask]], axis=1)
            qh = jnp.concatenate([qa[t], hot[...]], axis=0)
            sv = dot(ka, qh) * C2
            sc.at[pl.ds(sb, 5)][u] = sv
            mx.at[pl.ds(sb, 5)][u] = jnp.max(sv.reshape(CK // 8, 8, ROWS), axis=0)

        def o_step(i, sb, u):
            t, ch, e = dec(i)
            mo = mst[t]
            mn = jnp.maximum(mo, max8(mx.at[pl.ds(sb, 5)][u]))
            al = jnp.exp2(mo - mn)
            ev = jnp.exp2(sub8(sc.at[pl.ds(sb, 5)][u], mn))
            mst[t] = mn
            lst[t] = lst[t] * al + jnp.sum(ev, axis=0)
            ot[t] = (ot[t].reshape(-1, 8, ROWS) * al[None]).reshape(HEAD, ROWS) + dot(vt[e], ev.reshape(CK, ROWS).astype(BF))

        def pair(i, b, u):
            s_step(i + 1, start + b, u + 1)
            o_step(i, start + b, u)

        @pl.when(count > 0)
        def _():
            s_step(jnp.int32(0), start, 0)
            run(count, pair, lambda i, b, u: o_step(i, start + b, u))

    for t in range(6):
        landed(dor.at[t], tr.at[t, 2])
        dot_t[t] = dor[t].T
        l = sum8(lst[t])
        o = (ot[t].reshape(-1, 8, ROWS) / l[None]).reshape(HEAD, ROWS).astype(BF)
        qraw[t] = o.T
        dev = device(pos[t] // 2, x, par[t])
        send(qraw.at[t], att.at[seq_g[t // 2]], os_.at[t, 0], or_.at[seq_g[t // 2], 0], dev, me)
        dst[t] = sum8(jnp.sum((o.astype(F32) * dot_t[t].astype(F32)).reshape(-1, 8, ROWS), axis=0))
        mst[t] = mst[t] + jnp.log2(l)
        ot[t] = jnp.zeros((HEAD, ROWS), F32)

    def sum_core(units):
        for slot, h, n in units:
            @pl.when(n <= lims[slot])
            def _(slot=slot, n=n):
                remote(acc.at[ents(slot, n), :, 1 - c], peer.at[ents(slot, n)], as1.at[slot, n], ar1.at[slot, n], partner).start()

    def sum_x(units):
        for slot, h, n in units:
            @pl.when(n <= lims[slot])
            def _(slot=slot, h=h, n=n):
                es = ents(slot, n)
                landed(peer.at[es], ar1.at[slot, n])
                for v in range(HALF):
                    e = SLOT1 * slot + HALF * n + v
                    acc[e, :, c] += peer[e]
                one, other = (left, right) if h else (right, left)
                remote(acc.at[es, (x + 2) % 4, c], xr.at[2, es], as2.at[slot, n, 0], ar2.at[slot, n, 0], one).start()
                remote(acc.at[es, (x + 3 - 2 * h) % 4, c], xr.at[1 - h, es], as2.at[slot, n, 1], ar2.at[slot, n, 1], other).start()

    def sum_x2(units):
        for slot, h, n in units:
            @pl.when(n <= lims[slot])
            def _(slot=slot, h=h, n=n):
                es = ents(slot, n)
                to = (x + 1 + 2 * h) % 4
                landed(xr.at[2, es], ar2.at[slot, n, 0])
                acc[es, to, c] += xr[2, es]
                remote(acc.at[es, to, c], xr.at[h, es], as2.at[slot, n, 2], ar2.at[slot, n, 2], left if h else right).start()

    def sum_home(units):
        for slot, h, n in units:
            @pl.when(n <= lims[slot])
            def _(slot=slot, h=h, n=n):
                landed(xr.at[1 - h, ents(slot, n)], ar2.at[slot, n, 1])
                landed(xr.at[h, ents(slot, n)], ar2.at[slot, n, 2])
                for v in range(HALF):
                    to = HALF * n + v
                    e = SLOT1 * slot + to
                    zs[e] = acc[e, x, c] + xr[0, e] + xr[1, e]
                    send(zs.at[e], home.at[seqs[slot], nths[slot]], as3.at[e], ar3.at[seqs[slot], nths[slot]],
                         device(to, x, c), me)

    cum0 = phase(0)

    def upto(t, lo, hi):
        return jnp.minimum(jnp.maximum(nch[t] - lo, 0), hi - lo)

    @pl.loop(0, 7)
    def _(back):
        pc = jnp.maximum(3 - back, 0)
        lo = sel(back, [12, 8, 4, 2, 0, 0, 0])
        hi = sel(back, [16, 12, 8, 4, 2, 2, 2])
        starts = sel(pc, base[:PIECES])
        cum = phase(pc)
        steps = [jnp.int32(0)]
        for t in range(6):
            wanted = (back < 4) | (back == 4 + t // 2)
            steps.append(steps[-1] + jnp.where(wanted, upto(t, lo, hi), 0))
        count = steps[6]

        def dec(i):
            t = jnp.int32(0)
            for n in range(1, 6):
                t = t + (i >= steps[n]).astype(jnp.int32)
            ch = lo + i - sel(t, steps[:6])
            return t, ch, sel(t, ebase) + ch, starts + sel(t, cum[:6]) + ch - PP * pc

        def between():
            @pl.when((back >= 1) & (back <= 3))
            def _():
                @pl.when(back >= 2)
                def _():
                    sum_x2(halves(5 - back))
                sum_x(halves(4 - back))

            @pl.when(back == 4)
            def _():
                sum_home(halves(3))

            @pl.when(back == 5)
            def _():
                sum_x(half(0, 1))

            @pl.when(back == 6)
            def _():
                sum_x2(halves(1))
                sum_home(halves(2))

        def d_step(i, u):
            t, ch, e, si = dec(i)
            dp_ref[u % 2] = dot(values(e), dot_t[t])

        def g_step(i, u, ahead):
            t, ch, e, si = dec(i)
            pr = jnp.exp2(sub8(sc[si], mst[t]))
            prb = pr.reshape(CK, ROWS).astype(BF)
            acc[e, :, :, :, HEAD:] += dot(prb, dor[t]).reshape(4, 2, BLK, HEAD)
            ahead()
            ds = (pr * sub8(dp_ref[u % 2], dst[t])).reshape(CK, ROWS).astype(BF)
            ot[t] += dot(kt[e], ds)
            acc[e, :, :, :, :HEAD] += dot(ds, qn[t]).reshape(4, 2, BLK, HEAD)

        @pl.when(count > 0)
        def _():
            d_step(jnp.int32(0), 0)
            run(count, lambda i, b, u: g_step(i, u, lambda: d_step(i + 1, u + 1)),
                lambda i, b, u: g_step(i, u, lambda: None), between)
        @pl.when(back < 3)
        def _():
            sum_core(halves(pc))

        @pl.when(back == 3)
        def _():
            sum_core(half(0, 1))

        @pl.when(back == 6)
        def _():
            sum_core(half(0, 0))

        @pl.when(back >= 4)
        def _():
            for tl in range(2):
                t = 2 * (back - 4) + tl
                seq = sel(back - 4, seq_g)
                qn[t] = turn((ot[t] * SCALE).T, csr[t], -1)
                dev = device(sel(t, pos) // 2, x, sel(t, par))
                send(qn.at[t], gq.at[seq], os_.at[t, 1], or_.at[seq, 1], dev, me)

    sum_x(half(0, 0))
    sum_x2(half(0, 1))
    sum_home(halves(1))
    sum_x2(half(0, 0))
    sum_home(half(0, 1))
    sum_home(half(0, 0))
    for s in range(SEQS):
        for m, (chip, slot, last) in enumerate(CHIPS[s]):
            @pl.when(half_me <= last)
            def _(s=s, m=m):
                landed(home.at[s, m], ar3.at[s, m])

            @pl.when(half_me > last)
            def _(s=s, m=m):
                home[s, m] = jnp.zeros((BLK, TWO), F32)
        total = home[s, 0]
        for m in range(1, len(CHIPS[s])):
            total = total + home[s, m]
        dk = total[:, :HEAD] * SCALE
        other = jnp.concatenate([dk[:, HH:], dk[:, :HH]], axis=1)
        gk[s] = (dk * cos - other * sin).astype(BF)
        gv[s] = total[:, HEAD:].astype(BF)

    for s in range(SEQS):
        landed(att.at[s], or_.at[s, 0])
        landed(gq.at[s], or_.at[s, 1])
    n = 0
    for s in range(SEQS):
        for (chip, slot, last) in CHIPS[s]:
            @pl.when((half_me <= last) & (place != chip))
            def _(s=s, n=n):
                landed(kv.at[s], ks1.at[n])
            n += 1
    for s in range(SEQS):
        _, _, dev = work_of(s)

        @pl.when(dev != me)
        def _(s=s):
            landed(q.at[s], ts.at[s, 0])
            landed(csl, ts.at[s, 1])
            landed(do.at[s], ts.at[s, 2])
    for t in range(6):
        @pl.when(pos[t] != p)
        def _(t=t):
            landed(qraw.at[t], os_.at[t, 0])
            landed(qn.at[t], os_.at[t, 1])
    for slot in range(2):
        @pl.loop(0, lims[slot] + 1)
        def _(n, slot=slot):
            for d in range(3):
                landed(kvr.at[ents(slot, n), x, c], ks2.at[slot, n, d])
                landed(zs.at[ents(slot, n)], as2.at[slot, n, d])
            landed(kvr.at[ents(slot, n), :, c], ks3.at[slot, n])
            landed(peer.at[ents(slot, n)], as1.at[slot, n])
            for v in range(HALF):
                to = HALF * n + v

                @pl.when(to != place)
                def _(to=to):
                    landed(zs.at[SLOT1 * slot + to], as3.at[SLOT1 * slot + to])


def run_whole(q, do, key, value, pos32, freq):
    dma = pltpu.SemaphoreType.DMA
    n_kv = sum(len(c) for c in CHIPS)
    any_ = pl.BlockSpec(memory_space=pl.ANY)
    vm = pl.BlockSpec(memory_space=pltpu.VMEM)
    v = pltpu.VMEM
    return pl.pallas_call(
        whole_step,
        in_specs=[any_] * 5 + [vm], out_specs=[vm] * 4,
        out_shape=[v((6, ROWS, HEAD), BF), v((6, ROWS, HEAD), BF), v((6, BLK, HEAD), BF), v((6, BLK, HEAD), BF)],
        scratch_shapes=[
            v((6, ROWS, HEAD), BF), v((6, ROWS, HEAD), BF), v((6, BLK, HEAD), F32), v((ENT, 4, 2, BLK, TWO), BF),
            v((6, ROWS, HEAD), BF), v((6, HEAD, ROWS), BF), v((6, HEAD, ROWS), BF), v((HEAD, ROWS), BF), v((3, CK, HEAD), BF),
            v((ENT, HEAD, CK), BF), v((ENT, HEAD, CK), BF),
            v((SIDX, CK, ROWS), F32), v((SIDX, 8, ROWS), F32), v((6, 8, ROWS), F32), v((6, 8, ROWS), F32), v((6, 8, ROWS), F32),
            v((6, HEAD, ROWS), F32), v((2, CK, ROWS), F32), v((BLK, HEAD), F32),
            v((ENT, 4, 2, BLK, TWO), F32), v((ENT, 4, BLK, TWO), F32), v((3, ENT, BLK, TWO), F32), v((ENT, BLK, TWO), F32),
            v((SEQS, NCH, BLK, TWO), F32), v((SEQS, BLK, HEAD), BF), v((SEQS, BLK, TWO), BF), pltpu.SMEM((BLK,), jnp.int32),
            dma((n_kv,)), dma((2, HALVES)), dma((2, HALVES, 3)), dma((2, HALVES, 3)), dma((2, HALVES)), dma((2, HALVES)),
            dma((6, 3)), dma((6, 3)), dma((6, 2)), dma((6, 2)),
            dma((2, HALVES)), dma((2, HALVES)), dma((2, HALVES, 3)), dma((2, HALVES, 3)), dma((ENT,)), dma((SEQS, NCH)), dma(()), dma((2,))],
        compiler_params=pltpu.CompilerParams(has_side_effects=True, collective_id=0, vmem_limit_bytes=62500000),
        name='whole_step')(q, do, key, value, pos32, pltpu.with_memory_space_constraint(freq, pltpu.VMEM))


def put(*refs):
    here, there, sem = refs[:4], refs[4:8], refs[8]
    copies = [pltpu.make_async_copy(a, b, sem.at[n]) for n, (a, b) in enumerate(zip(here, there))]
    for copy in copies:
        copy.start()
    for copy in copies:
        copy.wait()


def run_put(*arrays):
    any_ = pl.BlockSpec(memory_space=pl.ANY)
    return pl.pallas_call(
        put, in_specs=[any_] * 4, out_specs=[any_] * 4,
        out_shape=[jax.ShapeDtypeStruct(a.shape, a.dtype) for a in arrays],
        scratch_shapes=[pltpu.SemaphoreType.DMA((4,))], name='put')(*[pltpu.with_memory_space_constraint(a, pltpu.VMEM) for a in arrays])


def solution(mesh):
    query_spec = PS('dp', 'cp', None, None)
    kv_spec = PS('dp', 'cp', None)
    pos_spec = PS(('dp', 'cp'))

    def per_device(query, key, value, positions, grad_out):
        inv_freq = jnp.power(jnp.float32(ROPE_BASE), -2.0 * jnp.arange(HH, dtype=F32) / HEAD)
        att, gq, gk, gv = run_whole(query.reshape(6, ROWS, HEAD), grad_out.reshape(6, ROWS, HEAD), key, value, positions, inv_freq[None])
        att, gq, gk, gv = run_put(att, gq, gk, gv)
        return att.reshape(query.shape), gq.reshape(query.shape), gk, gv

    return jax.shard_map(per_device, mesh=mesh, in_specs=(query_spec, kv_spec, kv_spec, pos_spec, query_spec),
                         out_specs=(query_spec, query_spec, kv_spec, kv_spec), check_vma=False)
```

time: 111 us -> 88.9 us (0.80)
  Pallas kernels: 102 us -> 88 us
  local copies, waits for them, and re-layouts: 5.24 us -> 0 us
  other arithmetic: 2.35 us -> 0.01 us
    pallas_call x1 -> x2, Pallas kernels: 102 us -> 88 us  [the longest x1 86.8 us: run_whole(): pl.pallas_call(whole_step, in_specs=[any_] * 5 + [vm], out_specs=[vm] * 4...]
    unnamed x14 -> x0, local copies, waits for them, and re-layouts: 5.24 us -> none
    concatenate x2 -> x0, other arithmetic: 1.43 us -> none  [the longest x1 0.74 us: per_device(): jnp.concatenate([(k1 * cos - k2 * sin).astype(BF), (k2 * cos + k1 * sin)....]
where the time goes in v3:
time: 88.9 us; the launch traced here: 88.7 us
  Pallas kernels  88 us (99%)
    pallas_call x1, Pallas kernels, run_whole(): pl.pallas_call(whole_step, in_specs=[any_] * 5 + [vm], out_specs=[vm] * 4...  86.8 us

profile of v3, /device:TPU:0, one launch (start us, length us, event | category | flops | bytes accessed | tf_op | source)
XLA Modules:
  0.0 88.7 jit_solution(8936885326899588797)
XLA Ops:
  0.6 86.8 %whole_step.1 = (bf16[6,512,128]{2,1,0:T(8,128)(2,1)S(1)}, bf16[6,512,128]{2,1,0:T(8,128)(2,1)S(1)}, bf16[6,32,128]{2,1,0:T(8,128)(2,1)S(1)}, bf16[6,32,128]{2,1,0:T(8,128)(2,1)S(1)}) custom-call(bf16[6,512,128]{2,1,0:T(8,128)(2,1)} %bitcast.4, bf16[6,512,128]{2,1,0:T(8,128)(2,1)} %bitcast.5, bf16[6,32,128]{2,1,0:T(8,128)(2,1)} %key.1, ...), custom_call_target="tpu_custom_call" | custom-call | tf_op jit(solution)/shard_map/whole_step/pallas_call | solution.py:616
  87.5 1.2 %put.1 = (bf16[6,512,128]{2,1,0:T(8,128)(2,1)}, bf16[6,512,128]{2,1,0:T(8,128)(2,1)}, bf16[6,32,128]{2,1,0:T(8,128)(2,1)}, bf16[6,32,128]{2,1,0:T(8,128)(2,1)}) custom-call(bf16[6,512,128]{2,1,0:T(8,128)(2,1)S(1)} %get-tuple-element.12.refs_0_, bf16[6,512,128]{2,1,0:T(8,128)(2,1)S(1)} %get-tuple-element.13.refs_1_, ...), custom_call_target="tpu_custom_call" | custom-call | tf_op jit(solution)/shard_map/put/pallas_call | solution.py:646
  (1 shorter events, 0.0 us)

commit v4 on v3

--- a/solution.py
+++ b/solution.py
@@ -9,8 +9,8 @@
 SEQS, HEADS, HEAD, BLK = 6, 16, 128, 32
 ROWS = BLK * HEADS
 CK = 256
-ENT = 24
-SLOT1 = 12
+ENT = 20
+SLOT1 = 10
 SIDX = 55
 SCALE = HEAD ** -0.5
 C2 = SCALE * 1.4426950408889634
@@ -21,12 +21,12 @@
 
 PLACE = [int(d, 16) for d in 'E47B1560328CDA9F']
 ORDER = [[int(d, 16) for d in row] for row in (
-    '5304218A67B9FDCE',
-    'EF69BA87215304DC',
-    'CEFDBA5498037126',
-    '169078BA4325DCFE',
-    'FE167980B53A42CD',
-    'CDFEB5894A173260')]
+    '5423018967BAFECD',
+    'EF8967BA542301DC',
+    'CDFEBA9854760123',
+    '1076982345BAFEDC',
+    'FE1076893245BACD',
+    'CDFEBA8945671032')]
 PIECES = 4
 PP = 16 // PIECES
 HALF = PP // 2
@@ -63,6 +63,9 @@
 
 
 DEST, CHIPS, LIM, SEQ, NTH, META = _tables()
+N_HOME = [sum(n // HALF <= last for row in CHIPS for _, _, last in row) for n in range(16)]
+N_KV = [N_HOME[n] - sum(n // HALF <= last for row in CHIPS for chip, _, last in row if chip == n) for n in range(16)]
+N_SUMS = [sum(HALF * (row[n] + 1) - (n < HALF * (row[n] + 1)) for row in LIM) for n in range(16)]
 NCH = max(len(c) for c in CHIPS)
 
 
@@ -125,6 +128,10 @@
     return out.astype(BF).reshape(ROWS, HEAD)
 
 
+def nr(slot, n):
+    return SLOT1 // HALF * slot + n
+
+
 def landed(ref, sem):
     pltpu.make_async_copy(ref, ref, sem).wait()
 
@@ -139,7 +146,7 @@
 def whole_step(q, do, key, value, pos32, freq, att, gq, gk, gv,
                qraw, dor, csr, kvr, qn, qa, dot_t, hot, mk, kt, vt, sc, mx, mst, lst, dst, ot, dp_ref, csl,
                acc, peer, xr, zs, home, keyl, kv, posl,
-               ks1, kr1, ks2, kr2, ks3, kr3, ts, tr, os_, or_, as1, ar1, as2, ar2, as3, ar3, cl, kl):
+               kr1, kr2, kr3, ts, tr, os_, ar1, ar2, s_one, s_x, s_core, or_, ar3, kl):
     me, c, x, place = place_of()
     p = 2 * place + c
     jme = jnp.minimum(p, 31 - p)
@@ -157,10 +164,17 @@
     ebase = [SLOT1 * slot_g[t // 2] for t in range(6)]
     partner = me + 1 - 2 * c
 
+    def landed_many(ref, counts, sem):
+        many = lut(place, counts)
+        for k in sorted(set(counts)):
+            @pl.when(many == k)
+            def _(k=k):
+                landed(ref.at[pl.ds(0, k)], sem)
+
     def remote(src, dst, ssem, rsem, dev):
         return pltpu.make_async_remote_copy(src, dst, ssem, rsem, device_id={'cp': dev}, device_id_type=MESH)
 
-    fetch = [pltpu.make_async_copy(pos32, posl, cl), pltpu.make_async_copy(key, keyl, kl.at[0]),
+    fetch = [pltpu.make_async_copy(pos32, posl, kl.at[2]), pltpu.make_async_copy(key, keyl, kl.at[0]),
              pltpu.make_async_copy(value, kv.at[:, :, HEAD:], kl.at[1])]
     for copy in fetch:
         copy.start()
@@ -211,15 +225,14 @@
     def send_do():
         for s in range(SEQS):
             _, k, dev = work_of(s)
-            send(do.at[s], dor.at[k], ts.at[s, 2], tr.at[k, 2], dev, me)
-
-    n = 0
+            send(do.at[s], dor.at[k], ts.at[s, 0], tr.at[k, 2], dev, me)
+
     for s in range(SEQS):
         for (chip, slot, last) in CHIPS[s]:
             @pl.when(half_me <= last)
-            def _(s=s, chip=chip, slot=slot, n=n):
-                send(kv.at[s], kvr.at[SLOT1 * slot + place, x, c], ks1.at[n], kr1.at[slot, half_me], device(chip, x, c), me)
-            n += 1
+            def _(s=s, chip=chip, slot=slot):
+                send(kv.at[s], kvr.at[SLOT1 * slot + place, x, c], s_one, kr1.at[nr(slot, half_me)], device(chip, x, c), me)
+    send_q()
 
     @pl.loop(0, ENT)
     def _(e):
@@ -246,8 +259,9 @@
         return [u for h in range(2) for u in half(i, h)]
 
     def half(i, h):
-        slots = 1 if isinstance(i, int) and i == PIECES - 1 else 2
+        slots = 1 if isinstance(i, int) and HALF * (2 * i + h) >= SLOT1 else 2
         return [(slot, h, 2 * i + h) for slot in range(slots)]
+
 
     def ents(slot, n):
         return pl.ds(SLOT1 * slot + HALF * n, HALF)
@@ -257,35 +271,33 @@
             @pl.when(n <= lims[slot])
             def _(slot=slot, n=n):
                 mine = kvr.at[ents(slot, n), x, c]
-                landed(mine, kr1.at[slot, n])
-                remote(mine, mine, ks2.at[slot, n, 0], kr2.at[slot, n, 0], right).start()
-                remote(mine, mine, ks2.at[slot, n, 1], kr2.at[slot, n, 1], left).start()
+                landed(mine, kr1.at[nr(slot, n)])
+                remote(mine, mine, s_x.at[nr(slot, n)], kr2.at[nr(slot, n), 0], right).start()
+                remote(mine, mine, s_x.at[nr(slot, n)], kr2.at[nr(slot, n), 1], left).start()
 
     def relay_x2(i):
         for slot, h, n in halves(i):
             @pl.when(n <= lims[slot])
             def _(slot=slot, h=h, n=n):
                 theirs = kvr.at[ents(slot, n), (x + 3 - 2 * h) % 4, c]
-                landed(theirs, kr2.at[slot, n, h])
-                remote(theirs, theirs, ks2.at[slot, n, 2], kr2.at[slot, n, 2], left if h else right).start()
+                landed(theirs, kr2.at[nr(slot, n), h])
+                remote(theirs, theirs, s_x.at[nr(slot, n)], kr2.at[nr(slot, n), 1 - h], left if h else right).start()
 
     def relay_core(i):
         for slot, h, n in halves(i):
             @pl.when(n <= lims[slot])
             def _(slot=slot, h=h, n=n):
-                landed(kvr.at[ents(slot, n), x, c], kr2.at[slot, n, 1 - h])
-                landed(kvr.at[ents(slot, n), x, c], kr2.at[slot, n, 2])
+                landed(kvr.at[ents(slot, n), pl.ds(0, 2), c], kr2.at[nr(slot, n), 1 - h])
                 both = kvr.at[ents(slot, n), :, c]
-                remote(both, both, ks3.at[slot, n], kr3.at[slot, n], partner).start()
+                remote(both, both, s_core.at[nr(slot, n)], kr3.at[nr(slot, n)], partner).start()
 
     relay_x(0)
     relay_x(1)
-    send_q()
+    relay_x2(0)
     relay_x(2)
+    relay_core(0)
+    relay_x2(1)
     relay_x(3)
-    relay_x2(0)
-    relay_x2(1)
-    relay_core(0)
 
     def prep_q(t):
         landed(qraw.at[t], tr.at[t, 0])
@@ -294,31 +306,23 @@
         qn[t] = rq
         qa[t] = rq.T
 
-    def phase(pc):
-        cum = [jnp.int32(0)]
-        for t in range(6):
-            cum.append(cum[-1] + jnp.minimum(jnp.maximum(nch[t] - PP * pc, 0), PP))
-        return cum
-
-    base = [jnp.int32(0)]
-    for pc in range(PIECES):
-        base.append(base[-1] + phase(pc)[6])
-
-    def segment(k):
-        pc = jnp.maximum(k - 2, 0)
-        cum = phase(pc)
-        part = jnp.minimum(k, 3)
-        first = sel(part, [cum[0], cum[2], cum[4], cum[0]])
-        count = sel(part, [cum[2], cum[4], cum[6], cum[6]]) - first
-
-        def dec(i):
-            i = i + first
-            t = jnp.int32(0)
-            for n in range(1, 6):
-                t = t + (i >= cum[n]).astype(jnp.int32)
-            ch = PP * pc + i - sel(t, cum[:6])
-            return t, ch, sel(t, ebase) + ch
-        return pc, sel(pc, base[:PIECES]) + first, count, dec
+    def upto(t, lo, hi):
+        return jnp.minimum(jnp.maximum(nch[t] - lo, 0), hi - lo)
+
+    def sums(counts):
+        out = [jnp.int32(0)]
+        for v in counts:
+            out.append(out[-1] + v)
+        return out
+
+    def tile_of(i, ends):
+        t = jnp.int32(0)
+        for n in range(1, 6):
+            t = t + (i >= ends[n]).astype(jnp.int32)
+        return t
+
+    low = sums([upto(t, 0, PP) for t in range(6)])
+    high = sums([upto(t, PP, 16) for t in range(6)])
 
     def run(count, pair, last, between=None):
         quads = (count - 1) // 4
@@ -353,8 +357,12 @@
     def values(e):
         return kvr[e, :, :, :, HEAD:].reshape(CK, HEAD)
 
-    @pl.loop(0, 6)
+    @pl.loop(0, 4)
     def _(k):
+        @pl.when((k >= 1) & (k <= 2))
+        def _():
+            relay_x2(k + 1)
+
         @pl.when((k >= 1) & (k <= 3))
         def _():
             relay_core(k)
@@ -362,20 +370,29 @@
         def _():
             prep_q(2 * k)
             prep_q(2 * k + 1)
-        @pl.when(k == 0)
+        @pl.when(k == 1)
         def _():
             send_do()
-            relay_x2(2)
-            relay_x2(3)
-        pc, start, count, dec = segment(k)
-        for slot, h, n in halves(pc):
-            @pl.when((n <= lims[slot]) & ((k == 0) | (k > 2)))
-            def _(slot=slot, n=n):
-                landed(kvr.at[ents(slot, n), :, 1 - c], kr3.at[slot, n])
-                for v in range(HALF):
-                    e = SLOT1 * slot + HALF * n + v
-                    kt[e] = keys(e).T
-                    vt[e] = values(e).T
+        for i in range(PIECES):
+            for slot, h, n in halves(i):
+                @pl.when((n <= lims[slot]) & (k == (0 if i == 0 else 3)))
+                def _(slot=slot, n=n):
+                    landed(kvr.at[ents(slot, n), :, 1 - c], kr3.at[nr(slot, n)])
+                    for v in range(HALF):
+                        e = SLOT1 * slot + HALF * n + v
+                        kt[e] = keys(e).T
+                        vt[e] = values(e).T
+
+        first = sel(k, [low[0], low[2], low[4], low[6]])
+        start = first
+        count = sel(k, [low[2], low[4], low[6], low[6] + high[6]]) - first
+
+        def dec(i):
+            i = i + jnp.where(k < 3, first, 0)
+            ends = [jnp.where(k < 3, low[t], high[t]) for t in range(6)]
+            t = tile_of(i, ends)
+            ch = jnp.where(k < 3, 0, PP) + i - sel(t, ends)
+            return t, ch, sel(t, ebase) + ch
 
         def s_step(i, sb, u):
             t, ch, e = dec(i)
@@ -405,6 +422,13 @@
             s_step(jnp.int32(0), start, 0)
             run(count, pair, lambda i, b, u: o_step(i, start + b, u))
 
+    landed_many(mx, N_KV, s_one)
+    for slot in range(2):
+        @pl.loop(0, lims[slot] + 1)
+        def _(n, slot=slot):
+            landed(kvr.at[ents(slot, n), pl.ds(0, 3), c], s_x.at[nr(slot, n)])
+            landed(kvr.at[ents(slot, n), :, c], s_core.at[nr(slot, n)])
+
     for t in range(6):
         landed(dor.at[t], tr.at[t, 2])
         dot_t[t] = dor[t].T
@@ -412,7 +436,7 @@
         o = (ot[t].reshape(-1, 8, ROWS) / l[None]).reshape(HEAD, ROWS).astype(BF)
         qraw[t] = o.T
         dev = device(pos[t] // 2, x, par[t])
-        send(qraw.at[t], att.at[seq_g[t // 2]], os_.at[t, 0], or_.at[seq_g[t // 2], 0], dev, me)
+        send(qraw.at[t], att.at[seq_g[t // 2]], os_.at[t], or_, dev, me)
         dst[t] = sum8(jnp.sum((o.astype(F32) * dot_t[t].astype(F32)).reshape(-1, 8, ROWS), axis=0))
         mst[t] = mst[t] + jnp.log2(l)
         ot[t] = jnp.zeros((HEAD, ROWS), F32)
@@ -421,20 +445,50 @@
         for slot, h, n in units:
             @pl.when(n <= lims[slot])
             def _(slot=slot, n=n):
-                remote(acc.at[ents(slot, n), :, 1 - c], peer.at[ents(slot, n)], as1.at[slot, n], ar1.at[slot, n], partner).start()
+                remote(acc.at[ents(slot, n), :, 1 - c], peer.at[ents(slot, n)], s_core.at[nr(slot, n)], ar1.at[nr(slot, n)], partner).start()
 
     def sum_x(units):
         for slot, h, n in units:
             @pl.when(n <= lims[slot])
             def _(slot=slot, h=h, n=n):
                 es = ents(slot, n)
-                landed(peer.at[es], ar1.at[slot, n])
-                for v in range(HALF):
-                    e = SLOT1 * slot + HALF * n + v
-                    acc[e, :, c] += peer[e]
+                add_peer(slot, n)
                 one, other = (left, right) if h else (right, left)
-                remote(acc.at[es, (x + 2) % 4, c], xr.at[2, es], as2.at[slot, n, 0], ar2.at[slot, n, 0], one).start()
-                remote(acc.at[es, (x + 3 - 2 * h) % 4, c], xr.at[1 - h, es], as2.at[slot, n, 1], ar2.at[slot, n, 1], other).start()
+                remote(acc.at[es, (x + 2) % 4, c], xr.at[2, es], s_x.at[nr(slot, n)], ar2.at[nr(slot, n), 0], one).start()
+                remote(acc.at[es, (x + 3 - 2 * h) % 4, c], xr.at[1 - h, es], s_x.at[nr(slot, n)], ar2.at[nr(slot, n), 1], other).start()
+
+    def add_peer(slot, n):
+        landed(peer.at[ents(slot, n)], ar1.at[nr(slot, n)])
+        for v in range(HALF):
+            e = SLOT1 * slot + HALF * n + v
+            acc[e, :, c] += peer[e]
+
+    def sum_direct(units):
+        for slot, h, n in units:
+            @pl.when(n <= lims[slot])
+            def _(slot=slot, n=n):
+                es = ents(slot, n)
+                add_peer(slot, n)
+                for d in range(3):
+                    to = (x + d + 1) % 4
+                    remote(acc.at[es, to, c], xr.at[d, es], s_x.at[nr(slot, n)], ar2.at[nr(slot, n), 1], device(place, to, c)).start()
+
+    def home_direct(units):
+        for slot, h, n in units:
+            @pl.when(n <= lims[slot])
+            def _(slot=slot, n=n):
+                landed(xr.at[:, ents(slot, n)], ar2.at[nr(slot, n), 1])
+                go_home(slot, n, (0, 1, 2))
+
+    def go_home(slot, n, parts):
+        for v in range(HALF):
+            to = HALF * n + v
+            e = SLOT1 * slot + to
+            total = acc[e, x, c]
+            for d in parts:
+                total = total + xr[d, e]
+            zs[e] = total
+            send(zs.at[e], home.at[seqs[slot], nths[slot]], s_one, ar3, device(to, x, c), me)
 
     def sum_x2(units):
         for slot, h, n in units:
@@ -442,68 +496,44 @@
             def _(slot=slot, h=h, n=n):
                 es = ents(slot, n)
                 to = (x + 1 + 2 * h) % 4
-                landed(xr.at[2, es], ar2.at[slot, n, 0])
+                landed(xr.at[2, es], ar2.at[nr(slot, n), 0])
                 acc[es, to, c] += xr[2, es]
-                remote(acc.at[es, to, c], xr.at[h, es], as2.at[slot, n, 2], ar2.at[slot, n, 2], left if h else right).start()
+                remote(acc.at[es, to, c], xr.at[h, es], s_x.at[nr(slot, n)], ar2.at[nr(slot, n), 1], left if h else right).start()
 
     def sum_home(units):
         for slot, h, n in units:
             @pl.when(n <= lims[slot])
             def _(slot=slot, h=h, n=n):
-                landed(xr.at[1 - h, ents(slot, n)], ar2.at[slot, n, 1])
-                landed(xr.at[h, ents(slot, n)], ar2.at[slot, n, 2])
-                for v in range(HALF):
-                    to = HALF * n + v
-                    e = SLOT1 * slot + to
-                    zs[e] = acc[e, x, c] + xr[0, e] + xr[1, e]
-                    send(zs.at[e], home.at[seqs[slot], nths[slot]], as3.at[e], ar3.at[seqs[slot], nths[slot]],
-                         device(to, x, c), me)
-
-    cum0 = phase(0)
-
-    def upto(t, lo, hi):
-        return jnp.minimum(jnp.maximum(nch[t] - lo, 0), hi - lo)
-
-    @pl.loop(0, 7)
+                landed(xr.at[pl.ds(0, 2), ents(slot, n)], ar2.at[nr(slot, n), 1])
+                go_home(slot, n, (0, 1))
+
+    at = [half(n // 2, n % 2) for n in range(HALVES)]
+    FROM = (12, 8, 2, 0, 4, 6)
+    CORE = (at[7] + at[6], at[5] + at[4], at[1], at[0], at[2], (), (), at[3])
+    HOOKS = (
+        (), ((sum_x, at[7] + at[6]),), ((sum_x2, at[7] + at[6]), (sum_x, at[5] + at[4])),
+        ((sum_x2, at[5] + at[4]), (sum_x, at[1])), ((sum_home, at[7] + at[6]), (sum_x2, at[1]), (sum_x, at[0])),
+        ((sum_home, at[5] + at[4]),), ((sum_x2, at[0]), (sum_direct, at[2])), ((sum_home, at[1]),))
+
+    @pl.loop(0, 8)
     def _(back):
-        pc = jnp.maximum(3 - back, 0)
-        lo = sel(back, [12, 8, 4, 2, 0, 0, 0])
-        hi = sel(back, [16, 12, 8, 4, 2, 2, 2])
-        starts = sel(pc, base[:PIECES])
-        cum = phase(pc)
-        steps = [jnp.int32(0)]
-        for t in range(6):
-            wanted = (back < 4) | (back == 4 + t // 2)
-            steps.append(steps[-1] + jnp.where(wanted, upto(t, lo, hi), 0))
+        lo = sel(jnp.minimum(back, 5), FROM)
+        hi = lo + jnp.where(back < 2, 4, 2)
+        steps = sums([jnp.where((back < 5) | (back == 5 + t // 2), upto(t, lo, hi), 0) for t in range(6)])
         count = steps[6]
 
         def dec(i):
-            t = jnp.int32(0)
-            for n in range(1, 6):
-                t = t + (i >= steps[n]).astype(jnp.int32)
+            t = tile_of(i, steps)
             ch = lo + i - sel(t, steps[:6])
-            return t, ch, sel(t, ebase) + ch, starts + sel(t, cum[:6]) + ch - PP * pc
+            where = jnp.where(lo < PP, sel(t, low[:6]), low[6] + sel(t, high[:6]) - PP)
+            return t, ch, sel(t, ebase) + ch, where + ch
 
         def between():
-            @pl.when((back >= 1) & (back <= 3))
-            def _():
-                @pl.when(back >= 2)
-                def _():
-                    sum_x2(halves(5 - back))
-                sum_x(halves(4 - back))
-
-            @pl.when(back == 4)
-            def _():
-                sum_home(halves(3))
-
-            @pl.when(back == 5)
-            def _():
-                sum_x(half(0, 1))
-
-            @pl.when(back == 6)
-            def _():
-                sum_x2(halves(1))
-                sum_home(halves(2))
+            for n in range(1, 8):
+                @pl.when(back == n)
+                def _(n=n):
+                    for job, units in HOOKS[n]:
+                        job(units)
 
         def d_step(i, u):
             t, ch, e, si = dec(i)
@@ -524,39 +554,34 @@
             d_step(jnp.int32(0), 0)
             run(count, lambda i, b, u: g_step(i, u, lambda: d_step(i + 1, u + 1)),
                 lambda i, b, u: g_step(i, u, lambda: None), between)
-        @pl.when(back < 3)
-        def _():
-            sum_core(halves(pc))
-
-        @pl.when(back == 3)
-        def _():
-            sum_core(half(0, 1))
-
-        @pl.when(back == 6)
-        def _():
-            sum_core(half(0, 0))
-
-        @pl.when(back >= 4)
+        for n in range(8):
+            @pl.when(back == n)
+            def _(n=n):
+                sum_core(CORE[n])
+
+        @pl.when(back >= 5)
         def _():
             for tl in range(2):
-                t = 2 * (back - 4) + tl
-                seq = sel(back - 4, seq_g)
+                t = 2 * (back - 5) + tl
+                seq = sel(back - 5, seq_g)
                 qn[t] = turn((ot[t] * SCALE).T, csr[t], -1)
                 dev = device(sel(t, pos) // 2, x, sel(t, par))
-                send(qn.at[t], gq.at[seq], os_.at[t, 1], or_.at[seq, 1], dev, me)
-
-    sum_x(half(0, 0))
-    sum_x2(half(0, 1))
-    sum_home(halves(1))
-    sum_x2(half(0, 0))
-    sum_home(half(0, 1))
-    sum_home(half(0, 0))
+                send(qn.at[t], gq.at[seq], os_.at[t], or_, dev, me)
+
+    sum_direct(at[3])
+    sum_home(at[0])
+    for s in range(SEQS):
+        _, _, dev = work_of(s)
+
+        @pl.when(dev != me)
+        def _(s=s):
+            landed(q.at[pl.ds(0, 2)], ts.at[s, 0])
+            landed(csl, ts.at[s, 1])
+    home_direct(at[2])
+    home_direct(at[3])
+    landed_many(zs, N_HOME, ar3)
     for s in range(SEQS):
         for m, (chip, slot, last) in enumerate(CHIPS[s]):
-            @pl.when(half_me <= last)
-            def _(s=s, m=m):
-                landed(home.at[s, m], ar3.at[s, m])
-
             @pl.when(half_me > last)
             def _(s=s, m=m):
                 home[s, m] = jnp.zeros((BLK, TWO), F32)
@@ -568,48 +593,22 @@
         gk[s] = (dk * cos - other * sin).astype(BF)
         gv[s] = total[:, HEAD:].astype(BF)
 
-    for s in range(SEQS):
-        landed(att.at[s], or_.at[s, 0])
-        landed(gq.at[s], or_.at[s, 1])
-    n = 0
-    for s in range(SEQS):
-        for (chip, slot, last) in CHIPS[s]:
-            @pl.when((half_me <= last) & (place != chip))
-            def _(s=s, n=n):
-                landed(kv.at[s], ks1.at[n])
-            n += 1
-    for s in range(SEQS):
-        _, _, dev = work_of(s)
-
-        @pl.when(dev != me)
-        def _(s=s):
-            landed(q.at[s], ts.at[s, 0])
-            landed(csl, ts.at[s, 1])
-            landed(do.at[s], ts.at[s, 2])
+    landed(sc.at[pl.ds(0, 3)], or_)
+    for slot in range(2):
+        @pl.loop(0, lims[slot] + 1)
+        def _(n, slot=slot):
+            landed(peer.at[ents(slot, n)], s_core.at[nr(slot, n)])
+            landed(xr.at[:, ents(slot, n)], s_x.at[nr(slot, n)])
+    landed_many(zs, N_SUMS, s_one)
     for t in range(6):
         @pl.when(pos[t] != p)
         def _(t=t):
-            landed(qraw.at[t], os_.at[t, 0])
-            landed(qn.at[t], os_.at[t, 1])
-    for slot in range(2):
-        @pl.loop(0, lims[slot] + 1)
-        def _(n, slot=slot):
-            for d in range(3):
-                landed(kvr.at[ents(slot, n), x, c], ks2.at[slot, n, d])
-                landed(zs.at[ents(slot, n)], as2.at[slot, n, d])
-            landed(kvr.at[ents(slot, n), :, c], ks3.at[slot, n])
-            landed(peer.at[ents(slot, n)], as1.at[slot, n])
-            for v in range(HALF):
-                to = HALF * n + v
-
-                @pl.when(to != place)
-                def _(to=to):
-                    landed(zs.at[SLOT1 * slot + to], as3.at[SLOT1 * slot + to])
+            landed(qraw.at[pl.ds(0, 2)], os_.at[t])
 
 
 def run_whole(q, do, key, value, pos32, freq):
     dma = pltpu.SemaphoreType.DMA
-    n_kv = sum(len(c) for c in CHIPS)
+    nh = ENT // HALF
     any_ = pl.BlockSpec(memory_space=pl.ANY)
     vm = pl.BlockSpec(memory_space=pltpu.VMEM)
     v = pltpu.VMEM
@@ -625,9 +624,8 @@
             v((6, HEAD, ROWS), F32), v((2, CK, ROWS), F32), v((BLK, HEAD), F32),
             v((ENT, 4, 2, BLK, TWO), F32), v((ENT, 4, BLK, TWO), F32), v((3, ENT, BLK, TWO), F32), v((ENT, BLK, TWO), F32),
             v((SEQS, NCH, BLK, TWO), F32), v((SEQS, BLK, HEAD), BF), v((SEQS, BLK, TWO), BF), pltpu.SMEM((BLK,), jnp.int32),
-            dma((n_kv,)), dma((2, HALVES)), dma((2, HALVES, 3)), dma((2, HALVES, 3)), dma((2, HALVES)), dma((2, HALVES)),
-            dma((6, 3)), dma((6, 3)), dma((6, 2)), dma((6, 2)),
-            dma((2, HALVES)), dma((2, HALVES)), dma((2, HALVES, 3)), dma((2, HALVES, 3)), dma((ENT,)), dma((SEQS, NCH)), dma(()), dma((2,))],
+            dma((nh,)), dma((nh, 2)), dma((nh,)), dma((6, 2)), dma((6, 3)), dma((6,)), dma((nh,)), dma((nh, 2)),
+            dma(()), dma((nh,)), dma((nh,)), dma(()), dma(()), dma((3,))],
         compiler_params=pltpu.CompilerParams(has_side_effects=True, collective_id=0, vmem_limit_bytes=62500000),
         name='whole_step')(q, do, key, value, pos32, pltpu.with_memory_space_constraint(freq, pltpu.VMEM))
 

time: 88.9 us -> 84.8 us (0.954)
  Pallas kernels: 88 us -> 83.5 us
    pallas_call x1, Pallas kernels: 86.8 us -> 82.3 us  [run_whole(): pl.pallas_call(whole_step, in_specs=[any_] * 5 + [vm], out_specs=[vm] * 4...]
where the time goes in v4:
time: 84.8 us; the launch traced here: 84.3 us
  Pallas kernels  83.5 us (98%)
    pallas_call x1, Pallas kernels, run_whole(): pl.pallas_call(whole_step, in_specs=[any_] * 5 + [vm], out_specs=[vm] * 4...  82.3 us

profile of v4, /device:TPU:0, one launch (start us, length us, event | category | flops | bytes accessed | tf_op | source)
XLA Modules:
  0.0 84.3 jit_solution(7440208350429433124)
XLA Ops:
  0.6 82.3 %whole_step.1 = (bf16[6,512,128]{2,1,0:T(8,128)(2,1)S(1)}, bf16[6,512,128]{2,1,0:T(8,128)(2,1)S(1)}, bf16[6,32,128]{2,1,0:T(8,128)(2,1)S(1)}, bf16[6,32,128]{2,1,0:T(8,128)(2,1)S(1)}) custom-call(bf16[6,512,128]{2,1,0:T(8,128)(2,1)} %bitcast.4, bf16[6,512,128]{2,1,0:T(8,128)(2,1)} %bitcast.5, bf16[6,32,128]{2,1,0:T(8,128)(2,1)} %key.1, ...), custom_call_target="tpu_custom_call" | custom-call | tf_op jit(solution)/shard_map/whole_step/pallas_call | solution.py:615
  82.9 1.2 %put.1 = (bf16[6,512,128]{2,1,0:T(8,128)(2,1)}, bf16[6,512,128]{2,1,0:T(8,128)(2,1)}, bf16[6,32,128]{2,1,0:T(8,128)(2,1)}, bf16[6,32,128]{2,1,0:T(8,128)(2,1)}) custom-call(bf16[6,512,128]{2,1,0:T(8,128)(2,1)S(1)} %get-tuple-element.12.refs_0_, bf16[6,512,128]{2,1,0:T(8,128)(2,1)S(1)} %get-tuple-element.13.refs_1_, ...), custom_call_target="tpu_custom_call" | custom-call | tf_op jit(solution)/shard_map/put/pallas_call | solution.py:644
  (1 shorter events, 0.0 us)

commit v5 on v4

--- a/solution.py
+++ b/solution.py
@@ -63,6 +63,7 @@
 
 
 DEST, CHIPS, LIM, SEQ, NTH, META = _tables()
+SWAP = [PLACE.index(n) // 8 for n in range(16)]
 N_HOME = [sum(n // HALF <= last for row in CHIPS for _, _, last in row) for n in range(16)]
 N_KV = [N_HOME[n] - sum(n // HALF <= last for row in CHIPS for chip, _, last in row if chip == n) for n in range(16)]
 N_SUMS = [sum(HALF * (row[n] + 1) - (n < HALF * (row[n] + 1)) for row in LIM) for n in range(16)]
@@ -100,8 +101,8 @@
     return jnp.dot(a, b, preferred_element_type=F32)
 
 
-def dot_nt(a, b):
-    return lax.dot_general(a, b, (((1,), (1,)), ((), ())), preferred_element_type=F32)
+def dot_tn(a, b):
+    return lax.dot_general(a, b, (((0,), (0,)), ((), ())), preferred_element_type=F32)
 
 
 def max8(v):
@@ -144,7 +145,7 @@
 
 
 def whole_step(q, do, key, value, pos32, freq, att, gq, gk, gv,
-               qraw, dor, csr, kvr, qn, qa, dot_t, hot, mk, kt, vt, sc, mx, mst, lst, dst, ot, dp_ref, csl,
+               qraw, dor, csr, kvr, qn, qa, dot_t, hot, mk, sc, mx, mst, lst, dst, ot, dp_ref, csl,
                acc, peer, xr, zs, home, keyl, kv, posl,
                kr1, kr2, kr3, ts, tr, os_, ar1, ar2, s_one, s_x, s_core, or_, ar3, kl):
     me, c, x, place = place_of()
@@ -260,7 +261,7 @@
 
     def half(i, h):
         slots = 1 if isinstance(i, int) and HALF * (2 * i + h) >= SLOT1 else 2
-        return [(slot, h, 2 * i + h) for slot in range(slots)]
+        return [(slot, (h + slot) % 2, 2 * i + h) for slot in range(slots)]
 
 
     def ents(slot, n):
@@ -321,28 +322,26 @@
             t = t + (i >= ends[n]).astype(jnp.int32)
         return t
 
-    low = sums([upto(t, 0, PP) for t in range(6)])
-    high = sums([upto(t, PP, 16) for t in range(6)])
-
-    def run(count, pair, last, between=None):
+    EDGES = (0, 4, 8, 16)
+    part = [sums([upto(t, EDGES[k], EDGES[k + 1]) for t in range(6)]) for k in range(3)]
+    begin = sums([ends[6] for ends in part])
+
+    def run(count, pair, last, between):
         quads = (count - 1) // 4
 
         def quad(b):
             for u in range(4):
                 pair(4 * b + u, 4 * b, u)
-        if between is None:
-            pl.loop(0, quads)(quad)
-        else:
-            @pl.loop(0, quads)
-            def _(b):
-                @pl.when(b == 2)
-                def _():
-                    between()
-                quad(b)
-
-            @pl.when(quads <= 2)
+        @pl.loop(0, quads)
+        def _(b):
+            @pl.when(b == 2)
             def _():
                 between()
+            quad(b)
+
+        @pl.when(quads <= 2)
+        def _():
+            between()
         rest = (count - 1) % 4
         for r in range(4):
             @pl.when(rest == r)
@@ -357,42 +356,40 @@
     def values(e):
         return kvr[e, :, :, :, HEAD:].reshape(CK, HEAD)
 
-    @pl.loop(0, 4)
+    @pl.loop(0, 6)
+    def _(t):
+        prep_q(t)
+
+    @pl.loop(0, 3)
     def _(k):
-        @pl.when((k >= 1) & (k <= 2))
+        @pl.when(k == 0)
         def _():
-            relay_x2(k + 1)
-
-        @pl.when((k >= 1) & (k <= 3))
-        def _():
-            relay_core(k)
-        @pl.when(k < 3)
-        def _():
-            prep_q(2 * k)
-            prep_q(2 * k + 1)
+            send_do()
+
         @pl.when(k == 1)
         def _():
-            send_do()
+            relay_core(2)
+            relay_core(3)
         for i in range(PIECES):
             for slot, h, n in halves(i):
-                @pl.when((n <= lims[slot]) & (k == (0 if i == 0 else 3)))
+                @pl.when((n <= lims[slot]) & (k == min(i, 2)))
                 def _(slot=slot, n=n):
                     landed(kvr.at[ents(slot, n), :, 1 - c], kr3.at[nr(slot, n)])
-                    for v in range(HALF):
-                        e = SLOT1 * slot + HALF * n + v
-                        kt[e] = keys(e).T
-                        vt[e] = values(e).T
-
-        first = sel(k, [low[0], low[2], low[4], low[6]])
-        start = first
-        count = sel(k, [low[2], low[4], low[6], low[6] + high[6]]) - first
+        ends = [sel(k, [part[n][t] for n in range(3)]) for t in range(7)]
+        start = sel(k, begin[:3])
+        count = ends[6]
 
         def dec(i):
-            i = i + jnp.where(k < 3, first, 0)
-            ends = [jnp.where(k < 3, low[t], high[t]) for t in range(6)]
             t = tile_of(i, ends)
-            ch = jnp.where(k < 3, 0, PP) + i - sel(t, ends)
+            ch = 4 * k + i - sel(t, ends[:6])
             return t, ch, sel(t, ebase) + ch
+
+        def between():
+            @pl.when(k == 0)
+            def _():
+                relay_x2(2)
+                relay_core(1)
+                relay_x2(3)
 
         def s_step(i, sb, u):
             t, ch, e = dec(i)
@@ -411,7 +408,7 @@
             ev = jnp.exp2(sub8(sc.at[pl.ds(sb, 5)][u], mn))
             mst[t] = mn
             lst[t] = lst[t] * al + jnp.sum(ev, axis=0)
-            ot[t] = (ot[t].reshape(-1, 8, ROWS) * al[None]).reshape(HEAD, ROWS) + dot(vt[e], ev.reshape(CK, ROWS).astype(BF))
+            ot[t] = (ot[t].reshape(-1, 8, ROWS) * al[None]).reshape(HEAD, ROWS) + dot_tn(values(e), ev.reshape(CK, ROWS).astype(BF))
 
         def pair(i, b, u):
             s_step(i + 1, start + b, u + 1)
@@ -420,7 +417,7 @@
         @pl.when(count > 0)
         def _():
             s_step(jnp.int32(0), start, 0)
-            run(count, pair, lambda i, b, u: o_step(i, start + b, u))
+            run(count, pair, lambda i, b, u: o_step(i, start + b, u), between)
 
     landed_many(mx, N_KV, s_one)
     for slot in range(2):
@@ -508,25 +505,39 @@
                 go_home(slot, n, (0, 1))
 
     at = [half(n // 2, n % 2) for n in range(HALVES)]
-    FROM = (12, 8, 2, 0, 4, 6)
-    CORE = (at[7] + at[6], at[5] + at[4], at[1], at[0], at[2], (), (), at[3])
+    swap = lut(place, SWAP)
+    last_but_one = [(slot, slot, 2 + swap) for slot in range(2)]
+    last = [(slot, 0, 3 - swap) for slot in range(2)]
+    FROM = (12, 8, 2, 0, 4 + 2 * swap, 6 - 2 * swap)
+    CORE = (at[7] + at[6], at[5] + at[4], at[1], at[0], last_but_one, (), (), last)
     HOOKS = (
-        (), ((sum_x, at[7] + at[6]),), ((sum_x2, at[7] + at[6]), (sum_x, at[5] + at[4])),
-        ((sum_x2, at[5] + at[4]), (sum_x, at[1])), ((sum_home, at[7] + at[6]), (sum_x2, at[1]), (sum_x, at[0])),
-        ((sum_home, at[5] + at[4]),), ((sum_x2, at[0]), (sum_direct, at[2])), ((sum_home, at[1]),))
-
-    @pl.loop(0, 8)
-    def _(back):
+        (), ((sum_x, at[7] + at[6]),), ((sum_x, at[5] + at[4]),), ((sum_x2, at[7] + at[6]), (sum_x, at[1])),
+        ((sum_x2, at[5] + at[4]), (sum_x, at[0])), ((sum_home, at[7] + at[6]), (sum_x2, at[1])),
+        ((sum_direct, last_but_one),), ((sum_x2, at[0]), (sum_home, at[5] + at[4])))
+
+    def segment(back):
         lo = sel(jnp.minimum(back, 5), FROM)
         hi = lo + jnp.where(back < 2, 4, 2)
         steps = sums([jnp.where((back < 5) | (back == 5 + t // 2), upto(t, lo, hi), 0) for t in range(6)])
-        count = steps[6]
 
         def dec(i):
             t = tile_of(i, steps)
             ch = lo + i - sel(t, steps[:6])
-            where = jnp.where(lo < PP, sel(t, low[:6]), low[6] + sel(t, high[:6]) - PP)
+            k = jnp.minimum(lo // 4, 2)
+            where = sel(k, [begin[n] + sel(t, part[n][:6]) - EDGES[n] for n in range(3)])
             return t, ch, sel(t, ebase) + ch, where + ch
+        return steps[6], dec
+
+    def d_step(u, t, ch, e, si):
+        dp_ref[u % 2] = dot(values(e), dot_t[t])
+
+    skip = segment(0)[0] == 0
+    d_step(0, *segment(skip.astype(jnp.int32))[1](0))
+
+    @pl.loop(0, 8)
+    def _(back):
+        count, dec = segment(back)
+        _, dec_next = segment(jnp.minimum(back + 1, 7))
 
         def between():
             for n in range(1, 8):
@@ -535,25 +546,24 @@
                     for job, units in HOOKS[n]:
                         job(units)
 
-        def d_step(i, u):
-            t, ch, e, si = dec(i)
-            dp_ref[u % 2] = dot(values(e), dot_t[t])
-
-        def g_step(i, u, ahead):
+        def g_step(i, u, ahead, after):
             t, ch, e, si = dec(i)
             pr = jnp.exp2(sub8(sc[si], mst[t]))
             prb = pr.reshape(CK, ROWS).astype(BF)
             acc[e, :, :, :, HEAD:] += dot(prb, dor[t]).reshape(4, 2, BLK, HEAD)
             ahead()
             ds = (pr * sub8(dp_ref[u % 2], dst[t])).reshape(CK, ROWS).astype(BF)
-            ot[t] += dot(kt[e], ds)
+            ot[t] += dot_tn(keys(e), ds)
             acc[e, :, :, :, :HEAD] += dot(ds, qn[t]).reshape(4, 2, BLK, HEAD)
+            after()
+
+        def nothing():
+            pass
 
         @pl.when(count > 0)
         def _():
-            d_step(jnp.int32(0), 0)
-            run(count, lambda i, b, u: g_step(i, u, lambda: d_step(i + 1, u + 1)),
-                lambda i, b, u: g_step(i, u, lambda: None), between)
+            run(count, lambda i, b, u: g_step(i, u, lambda: d_step(u + 1, *dec(i + 1)), nothing),
+                lambda i, b, u: g_step(i, u, nothing, lambda: d_step(0, *dec_next(0))), between)
         for n in range(8):
             @pl.when(back == n)
             def _(n=n):
@@ -568,7 +578,8 @@
                 dev = device(sel(t, pos) // 2, x, sel(t, par))
                 send(qn.at[t], gq.at[seq], os_.at[t], or_, dev, me)
 
-    sum_direct(at[3])
+    sum_direct(last)
+    sum_home(at[1])
     sum_home(at[0])
     for s in range(SEQS):
         _, _, dev = work_of(s)
@@ -577,8 +588,8 @@
         def _(s=s):
             landed(q.at[pl.ds(0, 2)], ts.at[s, 0])
             landed(csl, ts.at[s, 1])
-    home_direct(at[2])
-    home_direct(at[3])
+    home_direct(last_but_one)
+    home_direct(last)
     landed_many(zs, N_HOME, ar3)
     for s in range(SEQS):
         for m, (chip, slot, last) in enumerate(CHIPS[s]):
@@ -619,7 +630,6 @@
         scratch_shapes=[
             v((6, ROWS, HEAD), BF), v((6, ROWS, HEAD), BF), v((6, BLK, HEAD), F32), v((ENT, 4, 2, BLK, TWO), BF),
             v((6, ROWS, HEAD), BF), v((6, HEAD, ROWS), BF), v((6, HEAD, ROWS), BF), v((HEAD, ROWS), BF), v((3, CK, HEAD), BF),
-            v((ENT, HEAD, CK), BF), v((ENT, HEAD, CK), BF),
             v((SIDX, CK, ROWS), F32), v((SIDX, 8, ROWS), F32), v((6, 8, ROWS), F32), v((6, 8, ROWS), F32), v((6, 8, ROWS), F32),
             v((6, HEAD, ROWS), F32), v((2, CK, ROWS), F32), v((BLK, HEAD), F32),
             v((ENT, 4, 2, BLK, TWO), F32), v((ENT, 4, BLK, TWO), F32), v((3, ENT, BLK, TWO), F32), v((ENT, BLK, TWO), F32),

time: 84.8 us -> 80.3 us (0.947)
  Pallas kernels: 83.5 us -> 79.5 us
    pallas_call x1, Pallas kernels: 82.3 us -> 78.3 us  [run_whole(): pl.pallas_call(whole_step, in_specs=[any_] * 5 + [vm], out_specs=[vm] * 4...]
where the time goes in v5:
time: 80.3 us; the launch traced here: 80.2 us
  Pallas kernels  79.5 us (99%)
    pallas_call x1, Pallas kernels, run_whole(): pl.pallas_call(whole_step, in_specs=[any_] * 5 + [vm], out_specs=[vm] * 4...  78.3 us

profile of v5, /device:TPU:0, one launch (start us, length us, event | category | flops | bytes accessed | tf_op | source)
XLA Modules:
  0.0 80.2 jit_solution(855654680505513752)
XLA Ops:
  0.6 78.3 %whole_step.1 = (bf16[6,512,128]{2,1,0:T(8,128)(2,1)S(1)}, bf16[6,512,128]{2,1,0:T(8,128)(2,1)S(1)}, bf16[6,32,128]{2,1,0:T(8,128)(2,1)S(1)}, bf16[6,32,128]{2,1,0:T(8,128)(2,1)S(1)}) custom-call(bf16[6,512,128]{2,1,0:T(8,128)(2,1)} %bitcast.4, bf16[6,512,128]{2,1,0:T(8,128)(2,1)} %bitcast.5, bf16[6,32,128]{2,1,0:T(8,128)(2,1)} %key.1, ...), custom_call_target="tpu_custom_call" | custom-call | tf_op jit(solution)/shard_map/whole_step/pallas_call | solution.py:626
  79.0 1.2 %put.1 = (bf16[6,512,128]{2,1,0:T(8,128)(2,1)}, bf16[6,512,128]{2,1,0:T(8,128)(2,1)}, bf16[6,32,128]{2,1,0:T(8,128)(2,1)}, bf16[6,32,128]{2,1,0:T(8,128)(2,1)}) custom-call(bf16[6,512,128]{2,1,0:T(8,128)(2,1)S(1)} %get-tuple-element.12.refs_0_, bf16[6,512,128]{2,1,0:T(8,128)(2,1)S(1)} %get-tuple-element.13.refs_1_, ...), custom_call_target="tpu_custom_call" | custom-call | tf_op jit(solution)/shard_map/put/pallas_call | solution.py:654
  (1 shorter events, 0.0 us)
